TPU v7x, 128 devices: a whole 4x4x4 slice. The times are simulated.
128 devices in a mesh: grp: 4 (over z), tile: 32 (over x, y, core).
Axes of the slice: x: 4, y: 4, z: 4, core: 2. Of those that a mesh axis runs over, the one named last changes fastest.
Arguments:
- noise: bfloat16 [16, 3, 2048, 2048], P('grp', None, 'tile'), may hold values from -6 to 6
- stress: float32 [6, 2048, 2048], P(None, 'tile', 'grp'), as said below
- timescale: float32 [2048, 2048], P('tile', 'grp'), may hold values from 3 to 256
- mean_inflow: float32 [2048, 2048], P('tile', 'grp'), may hold values from 0.5 to 1.5
- courant: float32 [2048, 2048], P('tile', 'grp'), may hold values from 0.2 to 0.9
- prior_state: float32 [3, 2048, 2048], P(None, 'tile', 'grp'), may hold values from -6 to 6
- field: float32 [3, 8, 2048, 2048], P(None, None, 'tile', 'grp'), may hold values from -6 to 6
Outputs:
- inflow: bfloat16 [16, 3, 2048, 2048], P(None, None, 'tile', 'grp')
- field_out: float32 [3, 8, 2048, 2048], P(None, None, 'tile', 'grp')
Inputs may be any that keep to these rules, and one draw needn't show every extreme that they name: stress holds, per cell, R11, R21, R22, R31, R32, R33 of a symmetric positive definite tensor whose Cholesky factor has diagonal entries of 0.3 or more.
All inputs are finite; a program needn't handle non-finite values.
Results may differ from a plain program's by a relative error of at most 0.0085.
Values may be sent and summed in bfloat16 or wider, within the bound.
No kernel may reach another device: no remote copies, remote signals or barrier semaphores. Data moves between devices by JAX's collectives and lax.ppermute only.
A program may use at most 128 MiB of HBM per device.

v0:
```python
import math

import jax
import jax.numpy as jnp
import ml_dtypes
import numpy as np
from jax import lax
from jax.experimental import pallas as pl
from jax.experimental.pallas import tpu as pltpu
from jax.sharding import PartitionSpec as P


LS = 2
FW = 4
TAPS = 2 * FW + 1
CX = 8
BF16 = jnp.bfloat16
F32 = jnp.float32
SIDE = 4
AXES = ("grp", "tile")


def filter_taps():
    offsets = np.arange(-FW, FW + 1, dtype=np.float32)
    raw = np.exp(-math.pi * offsets * offsets / (2.0 * LS * LS)).astype(np.float32)
    return (raw / np.sqrt(np.sum(raw * raw))).astype(ml_dtypes.bfloat16)


def pick(taps, index):
    inside = (index >= 0) & (index < TAPS)
    return np.where(inside, taps.astype(np.float32)[np.clip(index, 0, TAPS - 1)], 0.0)


def filter_weights(per, comps, rows):
    taps = filter_taps()
    span = pick(taps, np.arange(256)[None, :] - np.arange(128)[:, None] - 64 + FW)
    row = np.arange(rows)
    inner = pick(taps, row[:, None] - row[None, :] + FW)
    outer = np.concatenate([np.arange(FW) - FW, rows + np.arange(FW)])
    edge = pick(taps, outer[:, None] - row[None, :] + FW)
    wide = 2 * FW
    own = np.zeros((2, comps * rows, 4 * rows), np.float32)
    halo = np.zeros((per, per * comps * wide, 4 * rows), np.float32)
    for i in range(per):
        for m in range(comps):
            q = m if m < 2 else 2 + i % 2
            own[i % 2, m * rows : (m + 1) * rows, q * rows : (q + 1) * rows] = inner
            top = (i * comps + m) * wide
            halo[i, top : top + wide, q * rows : (q + 1) * rows] = edge
    cast = lambda a: jnp.asarray(a.astype(ml_dtypes.bfloat16))
    return cast(span), cast(own), cast(halo)


TURNED = (((1,), (1,)), ((), ()))


def cost(flops, traffic):
    return pl.CostEstimate(flops=flops, bytes_accessed=traffic, transcendentals=0)


VMEM = pl.BlockSpec(memory_space=pltpu.VMEM)


def span_kernel(noise_ref, band_ref, out_ref):
    i = pl.program_id(0)
    windows = noise_ref.shape[2] // 128
    for w in range(windows):
        if w < windows - 1:
            window = noise_ref[0, :, 128 * w : 128 * w + 256]
        else:
            window = jnp.concatenate([noise_ref[0, :, 128 * w :], noise_ref[0, :, :128]], axis=-1)
        out_ref[i, 128 * w : 128 * w + 128] = lax.dot_general(
            band_ref[...], window, TURNED, preferred_element_type=F32
        ).astype(BF16)


def span_planes(noise, band):
    per, rows, length = noise.shape
    return pl.pallas_call(
        span_kernel,
        grid=(per,),
        in_specs=[pl.BlockSpec((1, rows, length), lambda i: (i, 0, 0)), VMEM],
        out_specs=VMEM,
        out_shape=jax.ShapeDtypeStruct((per, length, rows), BF16),
        compiler_params=pltpu.CompilerParams(vmem_limit_bytes=12 * 2**20),
        cost_estimate=cost(2 * 10**9, 4 * 10**6),
        name="span",
    )(noise, band)


ROUNDS = [(r, (d - r) % SIDE) for d in range(SIDE) for r in range(SIDE)]
SOON = 12


def seat():
    tile = lax.axis_index("tile")
    return lax.div(tile, 2 * SIDE), lax.rem(lax.div(tile, 2), SIDE), lax.rem(tile, 2), lax.axis_index("grp")


def rows_kernel(spans_ref, edges_ref, band_ref, own_ref, halo_ref, *refs):
    out_refs, done_ref = refs[:-1], refs[-1]
    per, length = spans_ref.shape[:2]
    windows, steps = 4, length // 512
    blocks = 2 * windows * steps
    band = band_ref[...]
    for step in range(steps):
        lo, hi = 512 * step, 512 * step + 640
        edges = edges_ref[:, lo:hi]
        if step == steps - 1:
            edges = jnp.concatenate([edges_ref[:, lo:], edges_ref[:, :128]], axis=-1)
        edge = jnp.concatenate(
            [
                lax.dot_general(
                    band, edges[:, 128 * v : 128 * v + 256], TURNED, preferred_element_type=F32
                ).astype(BF16)
                for v in range(windows)
            ],
            axis=0,
        )
        parts = [
            jnp.dot(spans_ref[i, lo : lo + 512], own_ref[i % 2], preferred_element_type=F32)
            + jnp.dot(edge, halo_ref[i], preferred_element_type=F32)
            for i in range(per)
        ]
        pairs = [part[:, :128] for part in parts]
        pairs += [parts[i][:, 128:] + parts[i + 1][:, 128:] for i in range(0, per, 2)]
        for k, pair in enumerate(pairs):
            pair = pair.astype(BF16)
            for v in range(2 * windows):
                done_ref[(2 * windows * step + 1 + v) % blocks, k] = pair[64 * v : 64 * (v + 1)]
    x, y, core, z = seat()
    for n, (r, d) in enumerate(ROUNDS):
        column = lax.rem(x - z + r + 2 * core + SIDE, SIDE)
        for h in range(2):
            target = (column * SIDE + lax.bitwise_xor(y, d)) * 2 + lax.rem(core + h, 2)
            out_refs[n][h] = done_ref[target]


def filter_rows(spans, halo, weights):
    block = (6, 64, 128)
    shapes = [(2,) + block] * len(ROUNDS)
    return pl.pallas_call(
        rows_kernel,
        in_specs=[VMEM] * 5,
        out_specs=[VMEM] * len(shapes),
        out_shape=[jax.ShapeDtypeStruct(a, BF16) for a in shapes],
        scratch_shapes=[pltpu.VMEM((4 * SIDE * 2,) + block, BF16)],
        compiler_params=pltpu.CompilerParams(vmem_limit_bytes=20 * 2**20),
        cost_estimate=cost(10**9, 4 * 10**6),
        name="rows",
    )(spans, halo, *weights)


def chain_kernel(*refs):
    count = len(ROUNDS)
    stay_refs, swap_refs = refs[:count], refs[count : count + 2]
    stress_ref, timescale_ref, mean_ref, courant_ref, prior_ref, field_ref = refs[count + 2 : count + 8]
    inflow_ref, result_ref, vel_ref, held_ref = refs[count + 8 :]
    groups, per = SIDE, 4
    depth = timescale_ref.shape[0]
    steps = groups * per
    low = lax.broadcasted_iota(jnp.int32, (depth, 128), 1) < 64
    x, y, core, z = seat()
    for n, (r, d) in enumerate(ROUNDS):
        for h in range(2):
            came = lax.rem(core + h, 2)
            time = lax.rem(z - x + r + 2 * came + SIDE, SIDE)
            if h == 0:
                held_ref[came, time, d] = stay_refs[n][0]
            else:
                held_ref[came, time, d] = swap_refs[0][n] if n < SOON else swap_refs[1][n - SOON]

    def band(d, _):
        lanes = pl.ds(pl.multiple_of(lax.bitwise_xor(y, d) * 128, 128), 128)
        courant = courant_ref[:, lanes]
        rest = 1.0 - courant
        inverse = 1.0 / rest
        decay = jnp.exp(-math.pi / (2.0 * timescale_ref[:, lanes]))
        gain = jnp.sqrt(1.0 - decay * decay)
        first = jnp.sqrt(stress_ref[0, :, lanes])
        second_low = stress_ref[1, :, lanes] / first
        second = jnp.sqrt(stress_ref[2, :, lanes] - second_low * second_low)
        third_low = stress_ref[3, :, lanes] / first
        third_mid = (stress_ref[4, :, lanes] - second_low * third_low) / second
        third = jnp.sqrt(stress_ref[5, :, lanes] - third_low * third_low - third_mid * third_mid)
        first, second_low, second = first * gain, second_low * gain, second * gain
        third_low, third_mid, third = third_low * gain, third_mid * gain, third * gain
        mean = mean_ref[:, lanes]
        phi = [prior_ref[m, :, lanes] / gain for m in range(3)]
        ratio = courant * inverse
        scale = ratio
        for g in range(groups):

            def pair(k):
                one, two = [held_ref[came, g, d, k].astype(F32) for came in range(2)]
                return jnp.where(low, one, pltpu.roll(two, 64, 1)), jnp.where(low, pltpu.roll(one, 64, 1), two)

            for half in range(2):
                third_planes = pair(4 + half)
                for i in range(2):
                    p = g * per + 2 * half + i
                    planes = (*pair(2 * half + i), third_planes[i])
                    phi = [decay * phi[m] + planes[m] for m in range(3)]
                    vel = (
                        mean + first * phi[0],
                        second_low * phi[0] + second * phi[1],
                        third_low * phi[0] + third_mid * phi[1] + third * phi[2],
                    )
                    for m in range(3):
                        inflow_ref[p, m, :, lanes] = vel[m].astype(BF16)
                        vel_ref[p, m] = vel[m] * scale
                    scale = scale * inverse
        back = rest / courant
        square = rest * rest
        square = square * square
        square = square * square
        last = square * square
        for m in range(3):
            power = None
            cells = []
            for j in range(CX):
                start = field_ref[m, j, :, lanes]
                cells.append(start if j == 0 else start * power)
                power = back if j == 0 else power * back
            for p in range(steps):
                inlet = vel_ref[p, m]
                cells = [cells[j] + (inlet if j == 0 else cells[j - 1]) for j in range(CX)]
            power = last
            for j in range(CX):
                result_ref[m, j, :, lanes] = cells[j] * power
                power = power * ratio
        return _

    lax.fori_loop(0, SIDE, band, 0)


def march_cells(stay, swap, stress, timescale, mean, courant, prior, field):
    rows = 16
    depth, length = timescale.shape
    steps = 16
    spec = lambda *lead: pl.BlockSpec(lead + (rows, length), lambda s: (0,) * len(lead) + (s, 0))
    return pl.pallas_call(
        chain_kernel,
        grid=(depth // rows,),
        in_specs=[pl.BlockSpec((1, 6, rows, 128), lambda s: (0, 0, s, 0))] * len(stay)
        + [pl.BlockSpec((part.shape[0], 6, rows, 128), lambda s: (0, 0, s, 0)) for part in swap]
        + [spec(6), spec(), spec(), spec(), spec(3), spec(3, CX)],
        out_specs=[spec(steps, 3), spec(3, CX)],
        out_shape=[
            jax.ShapeDtypeStruct((steps, 3, depth, length), BF16),
            jax.ShapeDtypeStruct((3, CX, depth, length), F32),
        ],
        scratch_shapes=[
            pltpu.VMEM((steps, 3, rows, 128), F32),
            pltpu.VMEM((2, SIDE, SIDE, 6, rows, 128), BF16),
        ],
        compiler_params=pltpu.CompilerParams(vmem_limit_bytes=32 * 2**20),
        cost_estimate=cost(10**9, 14 * 10**6),
        name="march",
    )(*stay, *swap, stress, timescale, mean, courant, prior, field)


def place(x, y, core, z):
    return z * 32 + (x * SIDE + y) * 2 + core


def moves(target):
    seats = [(x, y, core, z) for x in range(SIDE) for y in range(SIDE) for core in range(2) for z in range(SIDE)]
    return [(place(*one), place(*target(*one))) for one in seats]


def exchange(blocks):
    got = []
    for block, (r, d) in zip(blocks, ROUNDS, strict=True):
        pairs = moves(lambda x, y, core, z: ((x - z + r + 2 * core) % SIDE, y ^ d, core, x))
        got.append(lax.ppermute(block, AXES, pairs))
    return got


def body(noise, stress, timescale, mean_inflow, courant, prior_state, field):
    per, comps, rows, length = noise.shape
    tiles = lax.axis_size("tile")
    flat = noise.reshape(per * comps, rows, length)
    up = [(i, i + 1) for i in range(tiles - 1)]
    down = [(i + 1, i) for i in range(tiles - 1)]
    before = lax.ppermute(flat[:, rows - FW :], "tile", up)
    after = lax.ppermute(flat[:, :FW], "tile", down)
    halo = jnp.concatenate([before, after], axis=1).reshape(per * comps * 2 * FW, length)
    weights = filter_weights(per, comps, rows)
    spans = span_planes(noise.reshape(per, comps * rows, length), weights[0])
    other = moves(lambda x, y, core, z: (x, y, 1 - core, z))
    swap = []
    got = exchange(filter_rows(spans, halo, weights))
    for part in (got[:SOON], got[SOON:]):
        swap.append(lax.ppermute(jnp.stack([a[1] for a in part]), AXES, other))
    inflow, result = march_cells(got, swap, stress, timescale, mean_inflow, courant, prior_state, field)
    return (inflow, result)


def solution(mesh):
    placed = (
        P("grp", None, "tile", None),
        P(None, "tile", "grp"),
        P("tile", "grp"),
        P("tile", "grp"),
        P("tile", "grp"),
        P(None, "tile", "grp"),
        P(None, None, "tile", "grp"),
    )
    return jax.shard_map(
        body,
        mesh=mesh,
        in_specs=placed,
        out_specs=(P(None, None, "tile", "grp"), P(None, None, "tile", "grp")),
        check_vma=False,
    )
```

profile of v0, /device:TPU:1, one launch (start us, length us, event | category | flops | bytes accessed | tf_op | source)
XLA Modules:
  0.0 100.5 jit_solution(269002246426713508)
XLA Ops:
  0.6 1.3 %fusion = (bf16[12,4,2048]{2,1,0:T(4,128)(2,1)S(1)}, bf16[12,4,2048]{2,1,0:T(4,128)(2,1)S(1)}) fusion(bf16[12,64,2048]{2,1,0:T(8,128)(2,1)} %bitcast.4), kind=kLoop, calls=%fused_computation.14 | loop fusion | bytes 786432 | tf_op jit(solution)/shard_map/slice | solution.py:286
  2.0 4.6 %collective-permute-start = (bf16[12,4,2048]{2,1,0:T(4,128)(2,1)S(1)}, bf16[12,4,2048]{2,1,0:T(4,128)(2,1)S(1)}, u32[]{:S(2)}, u32[]{:S(2)}) collective-permute-start(bf16[12,4,2048]{2,1,0:T(4,128)(2,1)S(1)} %get-tuple-element.34), channel_id=1, source_target_pairs={{0,1},{1,2},{2,3},{3,4},{4,5},{5,6},{6,7},{7,8},{8,9},{9,10},{10,1... | collective-permute-start | bytes 589832 | tf_op jit(solution)/shard_map/ppermute | solution.py:286
  6.6 1.9 %collective-permute-start.1 = (bf16[12,4,2048]{2,1,0:T(4,128)(2,1)S(1)}, bf16[12,4,2048]{2,1,0:T(4,128)(2,1)S(1)}, u32[]{:S(2)}, u32[]{:S(2)}) collective-permute-start(bf16[12,4,2048]{2,1,0:T(4,128)(2,1)S(1)} %get-tuple-element.35), channel_id=1, source_target_pairs={{1,0},{2,1},{3,2},{4,3},{5,4},{6,5},{7,6},{8,7},{9,8},{10,9},{11,1... | collective-permute-start | bytes 589832 | tf_op jit(solution)/shard_map/ppermute | solution.py:287
  8.5 0.0 copy-start
  8.5 1.9 %copy-done = bf16[4,3,64,2048]{3,2,1,0:T(8,128)(2,1)S(1)} copy-done((bf16[4,3,64,2048]{3,2,1,0:T(8,128)(2,1)S(1)}, bf16[4,3,64,2048]{3,2,1,0:T(8,128)(2,1)}, u32[]{:S(2)}) %copy-start) | copy-done | bytes 3145752
  10.4 0.8 copy-done.4
  11.2 2.8 %span.1.spans_ref = bf16[4,2048,192]{2,1,0:T(8,128)(2,1)S(1)} custom-call(bf16[4,192,2048]{2,1,0:T(8,128)(2,1)S(1)} %bitcast.5, bf16[128,256]{1,0:T(8,128)(2,1)S(1)} %copy-done.4), custom_call_target="tpu_custom_call" | custom-call | flops 2000000000 | bytes 4000000 | tf_op jit(solution)/shard_map/span/pallas_call | solution.py:79
  14.0 0.2 maximum_bitcast_fusion.edges_ref
  14.3 3.1 %rows.1 = (bf16[2,6,64,128]{3,2,1,0:T(8,128)(2,1)S(1)}, bf16[2,6,64,128]{3,2,1,0:T(8,128)(2,1)S(1)}, bf16[2,6,64,128]{3,2,1,0:T(8,128)(2,1)S(1)}, bf16[2,6,64,12...) custom-call(bf16[4,2048,192]{2,1,0:T(8,128)(2,1)S(1)} %span.1.spans_, ...), custom_call_target="tpu_custom_call" | custom-call | flops 1000000000 | bytes 4000000 | tf_op jit(solution)/shard_map/rows/pallas_call | solution.py:142
  17.4 4.7 %collective-permute-start.2 = (bf16[2,6,64,128]{3,2,1,0:T(8,128)(2,1)S(1)}, bf16[2,6,64,128]{3,2,1,0:T(8,128)(2,1)S(1)}, u32[]{:S(2)}, u32[]{:S(2)}) collective-permute-start(bf16[2,6,64,128]{3,2,1,0:T(8,128)(2,1)S(1)} %get-tuple-element.18), channel_id=1, source_target_pairs={{0,0},{32,24},{64,16},{96,8},{1,17},{33,9},{65,1},{97,25},{2,2},{3... | collective-permute-start | bytes 589832 | tf_op jit(solution)/shard_map/ppermute | solution.py:276
  22.1 8.1 %collective-permute-start.3 = (bf16[2,6,64,128]{3,2,1,0:T(8,128)(2,1)S(1)}, bf16[2,6,64,128]{3,2,1,0:T(8,128)(2,1)S(1)}, u32[]{:S(2)}, u32[]{:S(2)}) collective-permute-start(bf16[2,6,64,128]{3,2,1,0:T(8,128)(2,1)S(1)} %get-tuple-element.19), channel_id=1, source_target_pairs={{0,14},{32,6},{64,30},{96,22},{1,31},{33,23},{65,15},{97,7},{2,12}... | collective-permute-start | bytes 589832 | tf_op jit(solution)/shard_map/ppermute | solution.py:276
  30.1 3.3 %collective-permute-start.6 = (bf16[2,6,64,128]{3,2,1,0:T(8,128)(2,1)S(1)}, bf16[2,6,64,128]{3,2,1,0:T(8,128)(2,1)S(1)}, u32[]{:S(2)}, u32[]{:S(2)}) collective-permute-start(bf16[2,6,64,128]{3,2,1,0:T(8,128)(2,1)S(1)} %get-tuple-element.22), channel_id=1, source_target_pairs={{0,2},{32,26},{64,18},{96,10},{1,19},{33,11},{65,3},{97,27},{2,0},... | collective-permute-start | bytes 589832 | tf_op jit(solution)/shard_map/ppermute | solution.py:276
  33.5 5.1 %collective-permute-start.7 = (bf16[2,6,64,128]{3,2,1,0:T(8,128)(2,1)S(1)}, bf16[2,6,64,128]{3,2,1,0:T(8,128)(2,1)S(1)}, u32[]{:S(2)}, u32[]{:S(2)}) collective-permute-start(bf16[2,6,64,128]{3,2,1,0:T(8,128)(2,1)S(1)} %get-tuple-element.23), channel_id=1, source_target_pairs={{0,8},{32,0},{64,24},{96,16},{1,25},{33,17},{65,9},{97,1},{2,10},{... | collective-permute-start | bytes 589832 | tf_op jit(solution)/shard_map/ppermute | solution.py:276
  38.6 0.1 collective-permute-start.8
  38.7 5.5 %collective-permute-done.4.refs_2_ = bf16[2,6,64,128]{3,2,1,0:T(8,128)(2,1)S(1)} collective-permute-done((bf16[2,6,64,128]{3,2,1,0:T(8,128)(2,1)S(1)}, bf16[2,6,64,128]{3,2,1,0:T(8,128)(2,1)S(1)}, u32[]{:S(2)}, u32[]{:S(2)}) %collective-permute-start.4) | collective-permute-done | bytes 196640 | tf_op jit(solution)/shard_map/ppermute | solution.py:276
  44.2 3.3 %collective-permute-start.10 = (bf16[2,6,64,128]{3,2,1,0:T(8,128)(2,1)S(1)}, bf16[2,6,64,128]{3,2,1,0:T(8,128)(2,1)S(1)}, u32[]{:S(2)}, u32[]{:S(2)}) collective-permute-start(bf16[2,6,64,128]{3,2,1,0:T(8,128)(2,1)S(1)} %get-tuple-element.26), channel_id=1, source_target_pairs={{0,4},{32,28},{64,20},{96,12},{1,21},{33,13},{65,5},{97,29},{2,6},... | collective-permute-start | bytes 589832 | tf_op jit(solution)/shard_map/ppermute | solution.py:276
  47.6 1.3 %collective-permute-start.11 = (bf16[2,6,64,128]{3,2,1,0:T(8,128)(2,1)S(1)}, bf16[2,6,64,128]{3,2,1,0:T(8,128)(2,1)S(1)}, u32[]{:S(2)}, u32[]{:S(2)}) collective-permute-start(bf16[2,6,64,128]{3,2,1,0:T(8,128)(2,1)S(1)} %get-tuple-element.27), channel_id=1, source_target_pairs={{0,10},{32,2},{64,26},{96,18},{1,27},{33,19},{65,11},{97,3},{2,8},... | collective-permute-start | bytes 589832 | tf_op jit(solution)/shard_map/ppermute | solution.py:276
  48.9 0.8 collective-permute-start.12
  49.8 4.3 %collective-permute-start.13 = (bf16[2,6,64,128]{3,2,1,0:T(8,128)(2,1)S(1)}, bf16[2,6,64,128]{3,2,1,0:T(8,128)(2,1)S(1)}, u32[]{:S(2)}, u32[]{:S(2)}) collective-permute-start(bf16[2,6,64,128]{3,2,1,0:T(8,128)(2,1)S(1)} %get-tuple-element.29), channel_id=1, source_target_pairs={{0,30},{32,22},{64,14},{96,6},{1,15},{33,7},{65,31},{97,23},{2,28}... | collective-permute-start | bytes 589832 | tf_op jit(solution)/shard_map/ppermute | solution.py:276
  54.1 7.0 %collective-permute-done.9.refs_7_ = bf16[2,6,64,128]{3,2,1,0:T(8,128)(2,1)S(1)} collective-permute-done((bf16[2,6,64,128]{3,2,1,0:T(8,128)(2,1)S(1)}, bf16[2,6,64,128]{3,2,1,0:T(8,128)(2,1)S(1)}, u32[]{:S(2)}, u32[]{:S(2)}) %collective-permute-start.9) | collective-permute-done | bytes 196640 | tf_op jit(solution)/shard_map/ppermute | solution.py:276
  61.2 1.6 %collective-permute-done.13.refs_11_ = bf16[2,6,64,128]{3,2,1,0:T(8,128)(2,1)S(1)} collective-permute-done((bf16[2,6,64,128]{3,2,1,0:T(8,128)(2,1)S(1)}, bf16[2,6,64,128]{3,2,1,0:T(8,128)(2,1)S(1)}, u32[]{:S(2)}, u32[]{:S(2)}) %collective-permute-start.13) | collective-permute-done | bytes 196640 | tf_op jit(solution)/shard_map/ppermute | solution.py:276
  62.7 7.9 %collective-permute-start.18 = (bf16[12,6,64,128]{3,2,1,0:T(8,128)(2,1)S(1)}, bf16[12,6,64,128]{3,2,1,0:T(8,128)(2,1)S(1)}, u32[]{:S(2)}, u32[]{:S(2)}) collective-permute-start(bf16[12,6,64,128]{3,2,1,0:T(8,128)(2,1)S(1)} %slice_dynamic-update-slice_fusion), channel_id=1, source_target_pairs={{0,1},{32,33},{64,65},{96,97},{1,0},{33,32},{65,64},{97,96},{2,3},... | collective-permute-start | bytes 3538952 | tf_op jit(solution)/shard_map/ppermute | solution.py:295
  70.6 1.7 %collective-permute-start.14 = (bf16[2,6,64,128]{3,2,1,0:T(8,128)(2,1)S(1)}, bf16[2,6,64,128]{3,2,1,0:T(8,128)(2,1)S(1)}, u32[]{:S(2)}, u32[]{:S(2)}) collective-permute-start(bf16[2,6,64,128]{3,2,1,0:T(8,128)(2,1)S(1)} %get-tuple-element.30), channel_id=1, source_target_pairs={{0,6},{32,30},{64,22},{96,14},{1,23},{33,15},{65,7},{97,31},{2,4},... | collective-permute-start | bytes 589832 | tf_op jit(solution)/shard_map/ppermute | solution.py:276
  72.4 5.3 %collective-permute-start.15 = (bf16[2,6,64,128]{3,2,1,0:T(8,128)(2,1)S(1)}, bf16[2,6,64,128]{3,2,1,0:T(8,128)(2,1)S(1)}, u32[]{:S(2)}, u32[]{:S(2)}) collective-permute-start(bf16[2,6,64,128]{3,2,1,0:T(8,128)(2,1)S(1)} %get-tuple-element.31), channel_id=1, source_target_pairs={{0,12},{32,4},{64,28},{96,20},{1,29},{33,21},{65,13},{97,5},{2,14}... | collective-permute-start | bytes 589832 | tf_op jit(solution)/shard_map/ppermute | solution.py:276
  77.7 3.3 %collective-permute-start.17 = (bf16[2,6,64,128]{3,2,1,0:T(8,128)(2,1)S(1)}, bf16[2,6,64,128]{3,2,1,0:T(8,128)(2,1)S(1)}, u32[]{:S(2)}, u32[]{:S(2)}) collective-permute-start(bf16[2,6,64,128]{3,2,1,0:T(8,128)(2,1)S(1)} %get-tuple-element.33), channel_id=1, source_target_pairs={{0,24},{32,16},{64,8},{96,0},{1,9},{33,1},{65,25},{97,17},{2,26},{... | collective-permute-start | bytes 589832 | tf_op jit(solution)/shard_map/ppermute | solution.py:276
  81.0 2.2 %collective-permute-done.15.refs_13_ = bf16[2,6,64,128]{3,2,1,0:T(8,128)(2,1)S(1)} collective-permute-done((bf16[2,6,64,128]{3,2,1,0:T(8,128)(2,1)S(1)}, bf16[2,6,64,128]{3,2,1,0:T(8,128)(2,1)S(1)}, u32[]{:S(2)}, u32[]{:S(2)}) %collective-permute-start.15) | collective-permute-done | bytes 196640 | tf_op jit(solution)/shard_map/ppermute | solution.py:276
  83.2 3.9 %collective-permute-done.16.refs_14_ = bf16[2,6,64,128]{3,2,1,0:T(8,128)(2,1)S(1)} collective-permute-done((bf16[2,6,64,128]{3,2,1,0:T(8,128)(2,1)S(1)}, bf16[2,6,64,128]{3,2,1,0:T(8,128)(2,1)S(1)}, u32[]{:S(2)}, u32[]{:S(2)}) %collective-permute-start.16) | collective-permute-done | bytes 196640 | tf_op jit(solution)/shard_map/ppermute | solution.py:276
  87.2 0.5 collective-permute-done.17.refs_15_
  87.6 0.1 pad_maximum_fusion
  87.7 3.6 %collective-permute-start.19 = (bf16[4,6,64,128]{3,2,1,0:T(8,128)(2,1)S(1)}, bf16[4,6,64,128]{3,2,1,0:T(8,128)(2,1)S(1)}, u32[]{:S(2)}, u32[]{:S(2)}) collective-permute-start(bf16[4,6,64,128]{3,2,1,0:T(8,128)(2,1)S(1)} %pad_maximum_fusion), channel_id=1, source_target_pairs={{0,1},{32,33},{64,65},{96,97},{1,0},{33,32},{65,64},{97,96},{2,3},... | collective-permute-start | bytes 1179656 | tf_op jit(solution)/shard_map/ppermute | solution.py:295
  91.3 1.3 %collective-permute-done.19.refs_17_ = bf16[4,6,64,128]{3,2,1,0:T(8,128)(2,1)S(1)} collective-permute-done((bf16[4,6,64,128]{3,2,1,0:T(8,128)(2,1)S(1)}, bf16[4,6,64,128]{3,2,1,0:T(8,128)(2,1)S(1)}, u32[]{:S(2)}, u32[]{:S(2)}) %collective-permute-start.19) | collective-permute-done | bytes 393248 | tf_op jit(solution)/shard_map/ppermute | solution.py:295
  92.7 7.8 %march.1 = (bf16[16,3,64,512]{3,2,1,0:T(8,128)(2,1)}, f32[3,8,64,512]{3,2,1,0:T(8,128)}) custom-call(bf16[2,6,64,128]{3,2,1,0:T(8,128)(2,1)S(1)} %collective-permute-done.2.refs_0_, bf16[2,6,64,128]{3,2,1,0:T(8,128)(2,1)S(1)} %collective-permute-done.3.refs_1_, bf16[2,6,64,128]{3,2,1,0:T(8,128)(2,1)S(1)} %collective-permute-done.4.refs_2_, ...), custom_call_target="tpu_custom_call" | custom-call | flops 1000000000 | bytes 14000000 | tf_op jit(solution)/shard_map/march/pallas_call | solution.py:242
  (52 shorter events, 0.3 us)
Async XLA Ops:
  2.0 12.0 %collective-permute-start = (bf16[12,4,2048]{2,1,0:T(4,128)(2,1)S(1)}, bf16[12,4,2048]{2,1,0:T(4,128)(2,1)S(1)}, u32[]{:S(2)}, u32[]{:S(2)}) collective-permute-start(bf16[12,4,2048]{2,1,0:T(4,128)(2,1)S(1)} %get-tuple-element.34), channel_id=1, source_target_pairs={{0,1},{1,2},{2,3},{3,4},{4,5},{5,6},{6,7},{7,8},{8,9},{9,10},{10,1... | collective-permute-start | bytes 589832 | tf_op jit(solution)/shard_map/ppermute | solution.py:286
  6.6 7.5 %collective-permute-start.1 = (bf16[12,4,2048]{2,1,0:T(4,128)(2,1)S(1)}, bf16[12,4,2048]{2,1,0:T(4,128)(2,1)S(1)}, u32[]{:S(2)}, u32[]{:S(2)}) collective-permute-start(bf16[12,4,2048]{2,1,0:T(4,128)(2,1)S(1)} %get-tuple-element.35), channel_id=1, source_target_pairs={{1,0},{2,1},{3,2},{4,3},{5,4},{6,5},{7,6},{8,7},{9,8},{10,9},{11,1... | collective-permute-start | bytes 589832 | tf_op jit(solution)/shard_map/ppermute | solution.py:287
  8.5 1.9 %copy-start = (bf16[4,3,64,2048]{3,2,1,0:T(8,128)(2,1)S(1)}, bf16[4,3,64,2048]{3,2,1,0:T(8,128)(2,1)}, u32[]{:S(2)}) copy-start(bf16[4,3,64,2048]{3,2,1,0:T(8,128)(2,1)} %param.10) | copy-start | bytes 9437188
  10.4 0.8 copy-start.4
  11.2 3.0 %copy-start.5 = (bf16[128,256]{1,0:T(8,128)(2,1)S(1)}, bf16[128,256]{1,0:T(8,128)(2,1)}, u32[]{:S(2)}) copy-start(bf16[128,256]{1,0:T(8,128)(2,1)} %constant.6.clone.band_ref) | copy-start | bytes 196612
  11.2 3.0 %copy-start.6 = (bf16[4,96,256]{2,1,0:T(8,128)(2,1)S(1)}, bf16[4,96,256]{2,1,0:T(8,128)(2,1)}, u32[]{:S(2)}) copy-start(bf16[4,96,256]{2,1,0:T(8,128)(2,1)} %constant.8.clone.halo_ref) | copy-start | bytes 589828
  11.2 3.0 %copy-start.7 = (bf16[2,192,256]{2,1,0:T(8,128)(2,1)S(1)}, bf16[2,192,256]{2,1,0:T(8,128)(2,1)}, u32[]{:S(2)}) copy-start(bf16[2,192,256]{2,1,0:T(8,128)(2,1)} %constant.7.clone.own_ref) | copy-start | bytes 589828
  14.2 78.4 %copy-start.3 = (f32[3,64,512]{2,1,0:T(8,128)S(1)}, f32[3,64,512]{2,1,0:T(8,128)}, u32[]{:S(2)}) copy-start(f32[3,64,512]{2,1,0:T(8,128)} %refs_22_.1) | copy-start | bytes 1179652
  14.3 78.4 %copy-start.8 = (f32[64,512]{1,0:T(8,128)S(1)}, f32[64,512]{1,0:T(8,128)}, u32[]{:S(2)}) copy-start(f32[64,512]{1,0:T(8,128)} %refs_19_.1) | copy-start | bytes 393220
  14.3 78.4 %copy-start.9 = (f32[64,512]{1,0:T(8,128)S(1)}, f32[64,512]{1,0:T(8,128)}, u32[]{:S(2)}) copy-start(f32[64,512]{1,0:T(8,128)} %refs_20_.1) | copy-start | bytes 393220
  14.3 78.4 %copy-start.10 = (f32[64,512]{1,0:T(8,128)S(1)}, f32[64,512]{1,0:T(8,128)}, u32[]{:S(2)}) copy-start(f32[64,512]{1,0:T(8,128)} %refs_21_.1) | copy-start | bytes 393220
  17.4 16.1 %collective-permute-start.2 = (bf16[2,6,64,128]{3,2,1,0:T(8,128)(2,1)S(1)}, bf16[2,6,64,128]{3,2,1,0:T(8,128)(2,1)S(1)}, u32[]{:S(2)}, u32[]{:S(2)}) collective-permute-start(bf16[2,6,64,128]{3,2,1,0:T(8,128)(2,1)S(1)} %get-tuple-element.18), channel_id=1, source_target_pairs={{0,0},{32,24},{64,16},{96,8},{1,17},{33,9},{65,1},{97,25},{2,2},{3... | collective-permute-start | bytes 589832 | tf_op jit(solution)/shard_map/ppermute | solution.py:276
  22.1 16.5 %collective-permute-start.3 = (bf16[2,6,64,128]{3,2,1,0:T(8,128)(2,1)S(1)}, bf16[2,6,64,128]{3,2,1,0:T(8,128)(2,1)S(1)}, u32[]{:S(2)}, u32[]{:S(2)}) collective-permute-start(bf16[2,6,64,128]{3,2,1,0:T(8,128)(2,1)S(1)} %get-tuple-element.19), channel_id=1, source_target_pairs={{0,14},{32,6},{64,30},{96,22},{1,31},{33,23},{65,15},{97,7},{2,12}... | collective-permute-start | bytes 589832 | tf_op jit(solution)/shard_map/ppermute | solution.py:276
  30.1 14.1 %collective-permute-start.4 = (bf16[2,6,64,128]{3,2,1,0:T(8,128)(2,1)S(1)}, bf16[2,6,64,128]{3,2,1,0:T(8,128)(2,1)S(1)}, u32[]{:S(2)}, u32[]{:S(2)}) collective-permute-start(bf16[2,6,64,128]{3,2,1,0:T(8,128)(2,1)S(1)} %get-tuple-element.20), channel_id=1, source_target_pairs={{0,20},{32,12},{64,4},{96,28},{1,5},{33,29},{65,21},{97,13},{2,22}... | collective-permute-start | bytes 589832 | tf_op jit(solution)/shard_map/ppermute | solution.py:276
  30.1 14.1 %collective-permute-start.5 = (bf16[2,6,64,128]{3,2,1,0:T(8,128)(2,1)S(1)}, bf16[2,6,64,128]{3,2,1,0:T(8,128)(2,1)S(1)}, u32[]{:S(2)}, u32[]{:S(2)}) collective-permute-start(bf16[2,6,64,128]{3,2,1,0:T(8,128)(2,1)S(1)} %get-tuple-element.21), channel_id=1, source_target_pairs={{0,26},{32,18},{64,10},{96,2},{1,11},{33,3},{65,27},{97,19},{2,24}... | collective-permute-start | bytes 589832 | tf_op jit(solution)/shard_map/ppermute | solution.py:276
  30.1 17.5 %collective-permute-start.6 = (bf16[2,6,64,128]{3,2,1,0:T(8,128)(2,1)S(1)}, bf16[2,6,64,128]{3,2,1,0:T(8,128)(2,1)S(1)}, u32[]{:S(2)}, u32[]{:S(2)}) collective-permute-start(bf16[2,6,64,128]{3,2,1,0:T(8,128)(2,1)S(1)} %get-tuple-element.22), channel_id=1, source_target_pairs={{0,2},{32,26},{64,18},{96,10},{1,19},{33,11},{65,3},{97,27},{2,0},... | collective-permute-start | bytes 589832 | tf_op jit(solution)/shard_map/ppermute | solution.py:276
  33.5 15.5 %collective-permute-start.7 = (bf16[2,6,64,128]{3,2,1,0:T(8,128)(2,1)S(1)}, bf16[2,6,64,128]{3,2,1,0:T(8,128)(2,1)S(1)}, u32[]{:S(2)}, u32[]{:S(2)}) collective-permute-start(bf16[2,6,64,128]{3,2,1,0:T(8,128)(2,1)S(1)} %get-tuple-element.23), channel_id=1, source_target_pairs={{0,8},{32,0},{64,24},{96,16},{1,25},{33,17},{65,9},{97,1},{2,10},{... | collective-permute-start | bytes 589832 | tf_op jit(solution)/shard_map/ppermute | solution.py:276
  38.5 54.2 %copy-start.2 = (f32[6,64,512]{2,1,0:T(8,128)S(1)}, f32[6,64,512]{2,1,0:T(8,128)}, u32[]{:S(2)}) copy-start(f32[6,64,512]{2,1,0:T(8,128)} %refs_18_.1) | copy-start | bytes 2359300
  38.6 11.2 %collective-permute-start.8 = (bf16[2,6,64,128]{3,2,1,0:T(8,128)(2,1)S(1)}, bf16[2,6,64,128]{3,2,1,0:T(8,128)(2,1)S(1)}, u32[]{:S(2)}, u32[]{:S(2)}) collective-permute-start(bf16[2,6,64,128]{3,2,1,0:T(8,128)(2,1)S(1)} %get-tuple-element.24), channel_id=1, source_target_pairs={{0,22},{32,14},{64,6},{96,30},{1,7},{33,31},{65,23},{97,15},{2,20}... | collective-permute-start | bytes 589832 | tf_op jit(solution)/shard_map/ppermute | solution.py:276
  44.2 16.8 %collective-permute-start.9 = (bf16[2,6,64,128]{3,2,1,0:T(8,128)(2,1)S(1)}, bf16[2,6,64,128]{3,2,1,0:T(8,128)(2,1)S(1)}, u32[]{:S(2)}, u32[]{:S(2)}) collective-permute-start(bf16[2,6,64,128]{3,2,1,0:T(8,128)(2,1)S(1)} %get-tuple-element.25), channel_id=1, source_target_pairs={{0,28},{32,20},{64,12},{96,4},{1,13},{33,5},{65,29},{97,21},{2,30}... | collective-permute-start | bytes 589832 | tf_op jit(solution)/shard_map/ppermute | solution.py:276
  44.2 16.8 %collective-permute-start.10 = (bf16[2,6,64,128]{3,2,1,0:T(8,128)(2,1)S(1)}, bf16[2,6,64,128]{3,2,1,0:T(8,128)(2,1)S(1)}, u32[]{:S(2)}, u32[]{:S(2)}) collective-permute-start(bf16[2,6,64,128]{3,2,1,0:T(8,128)(2,1)S(1)} %get-tuple-element.26), channel_id=1, source_target_pairs={{0,4},{32,28},{64,20},{96,12},{1,21},{33,13},{65,5},{97,29},{2,6},... | collective-permute-start | bytes 589832 | tf_op jit(solution)/shard_map/ppermute | solution.py:276
  47.6 13.5 %collective-permute-start.11 = (bf16[2,6,64,128]{3,2,1,0:T(8,128)(2,1)S(1)}, bf16[2,6,64,128]{3,2,1,0:T(8,128)(2,1)S(1)}, u32[]{:S(2)}, u32[]{:S(2)}) collective-permute-start(bf16[2,6,64,128]{3,2,1,0:T(8,128)(2,1)S(1)} %get-tuple-element.27), channel_id=1, source_target_pairs={{0,10},{32,2},{64,26},{96,18},{1,27},{33,19},{65,11},{97,3},{2,8},... | collective-permute-start | bytes 589832 | tf_op jit(solution)/shard_map/ppermute | solution.py:276
  48.9 43.8 %copy-start.1 = (f32[3,8,64,512]{3,2,1,0:T(8,128)S(1)}, f32[3,8,64,512]{3,2,1,0:T(8,128)}, u32[]{:S(2)}) copy-start(f32[3,8,64,512]{3,2,1,0:T(8,128)} %refs_23_.1) | copy-start | bytes 9437188
  48.9 12.2 %collective-permute-start.12 = (bf16[2,6,64,128]{3,2,1,0:T(8,128)(2,1)S(1)}, bf16[2,6,64,128]{3,2,1,0:T(8,128)(2,1)S(1)}, u32[]{:S(2)}, u32[]{:S(2)}) collective-permute-start(bf16[2,6,64,128]{3,2,1,0:T(8,128)(2,1)S(1)} %get-tuple-element.28), channel_id=1, source_target_pairs={{0,16},{32,8},{64,0},{96,24},{1,1},{33,25},{65,17},{97,9},{2,18},{... | collective-permute-start | bytes 589832 | tf_op jit(solution)/shard_map/ppermute | solution.py:276
  49.8 12.9 %collective-permute-start.13 = (bf16[2,6,64,128]{3,2,1,0:T(8,128)(2,1)S(1)}, bf16[2,6,64,128]{3,2,1,0:T(8,128)(2,1)S(1)}, u32[]{:S(2)}, u32[]{:S(2)}) collective-permute-start(bf16[2,6,64,128]{3,2,1,0:T(8,128)(2,1)S(1)} %get-tuple-element.29), channel_id=1, source_target_pairs={{0,30},{32,22},{64,14},{96,6},{1,15},{33,7},{65,31},{97,23},{2,28}... | collective-permute-start | bytes 589832 | tf_op jit(solution)/shard_map/ppermute | solution.py:276
  62.7 29.9 %collective-permute-start.18 = (bf16[12,6,64,128]{3,2,1,0:T(8,128)(2,1)S(1)}, bf16[12,6,64,128]{3,2,1,0:T(8,128)(2,1)S(1)}, u32[]{:S(2)}, u32[]{:S(2)}) collective-permute-start(bf16[12,6,64,128]{3,2,1,0:T(8,128)(2,1)S(1)} %slice_dynamic-update-slice_fusion), channel_id=1, source_target_pairs={{0,1},{32,33},{64,65},{96,97},{1,0},{33,32},{65,64},{97,96},{2,3},... | collective-permute-start | bytes 3538952 | tf_op jit(solution)/shard_map/ppermute | solution.py:295
  70.6 10.4 %collective-permute-start.14 = (bf16[2,6,64,128]{3,2,1,0:T(8,128)(2,1)S(1)}, bf16[2,6,64,128]{3,2,1,0:T(8,128)(2,1)S(1)}, u32[]{:S(2)}, u32[]{:S(2)}) collective-permute-start(bf16[2,6,64,128]{3,2,1,0:T(8,128)(2,1)S(1)} %get-tuple-element.30), channel_id=1, source_target_pairs={{0,6},{32,30},{64,22},{96,14},{1,23},{33,15},{65,7},{97,31},{2,4},... | collective-permute-start | bytes 589832 | tf_op jit(solution)/shard_map/ppermute | solution.py:276
  72.4 10.9 %collective-permute-start.15 = (bf16[2,6,64,128]{3,2,1,0:T(8,128)(2,1)S(1)}, bf16[2,6,64,128]{3,2,1,0:T(8,128)(2,1)S(1)}, u32[]{:S(2)}, u32[]{:S(2)}) collective-permute-start(bf16[2,6,64,128]{3,2,1,0:T(8,128)(2,1)S(1)} %get-tuple-element.31), channel_id=1, source_target_pairs={{0,12},{32,4},{64,28},{96,20},{1,29},{33,21},{65,13},{97,5},{2,14}... | collective-permute-start | bytes 589832 | tf_op jit(solution)/shard_map/ppermute | solution.py:276
  77.7 9.4 %collective-permute-start.16 = (bf16[2,6,64,128]{3,2,1,0:T(8,128)(2,1)S(1)}, bf16[2,6,64,128]{3,2,1,0:T(8,128)(2,1)S(1)}, u32[]{:S(2)}, u32[]{:S(2)}) collective-permute-start(bf16[2,6,64,128]{3,2,1,0:T(8,128)(2,1)S(1)} %get-tuple-element.32), channel_id=1, source_target_pairs={{0,18},{32,10},{64,2},{96,26},{1,3},{33,27},{65,19},{97,11},{2,16}... | collective-permute-start | bytes 589832 | tf_op jit(solution)/shard_map/ppermute | solution.py:276
  77.7 9.9 %collective-permute-start.17 = (bf16[2,6,64,128]{3,2,1,0:T(8,128)(2,1)S(1)}, bf16[2,6,64,128]{3,2,1,0:T(8,128)(2,1)S(1)}, u32[]{:S(2)}, u32[]{:S(2)}) collective-permute-start(bf16[2,6,64,128]{3,2,1,0:T(8,128)(2,1)S(1)} %get-tuple-element.33), channel_id=1, source_target_pairs={{0,24},{32,16},{64,8},{96,0},{1,9},{33,1},{65,25},{97,17},{2,26},{... | collective-permute-start | bytes 589832 | tf_op jit(solution)/shard_map/ppermute | solution.py:276
  87.7 5.0 %collective-permute-start.19 = (bf16[4,6,64,128]{3,2,1,0:T(8,128)(2,1)S(1)}, bf16[4,6,64,128]{3,2,1,0:T(8,128)(2,1)S(1)}, u32[]{:S(2)}, u32[]{:S(2)}) collective-permute-start(bf16[4,6,64,128]{3,2,1,0:T(8,128)(2,1)S(1)} %pad_maximum_fusion), channel_id=1, source_target_pairs={{0,1},{32,33},{64,65},{96,97},{1,0},{33,32},{65,64},{97,96},{2,3},... | collective-permute-start | bytes 1179656 | tf_op jit(solution)/shard_map/ppermute | solution.py:295
where the time goes:
time: 101 us
  starting transfers between devices  59.3 us (59%)
  waiting for transfers between devices  22 us (22%)
  Pallas kernels  13.6 us (13%)
  local copies, waits for them, and re-layouts  4.29 us (4%)
  between operations  1.01 us (1%)
    ppermute x16, starting transfers between devices, exchange(): got.append(lax.ppermute(block, AXES, pairs))  41.3 us
    ppermute x16, waiting for transfers between devices, exchange(): got.append(lax.ppermute(block, AXES, pairs))  20.7 us
    ppermute x2, starting transfers between devices, body(): swap.append(lax.ppermute(jnp.stack([a[1] for a in part]), AXES, other))  11.5 us
    pallas_call x1, Pallas kernels, march_cells(): pl.pallas_call(chain_kernel, grid=(depth // rows,), in_specs=[pl.BlockSpe...  7.79 us
    ppermute x1, starting transfers between devices, body(): before = lax.ppermute(flat[:, rows - FW:], 'tile', up)  4.58 us
    pallas_call x1, Pallas kernels, filter_rows(): pl.pallas_call(rows_kernel, in_specs=[VMEM] * 5, out_specs=[VMEM] * len(s...  3.1 us
    unnamed x33, local copies, waits for them, and re-layouts  2.92 us
    pallas_call x1, Pallas kernels, span_planes(): pl.pallas_call(span_kernel, grid=(per,), in_specs=[pl.BlockSpec((1, rows,...  2.76 us
  transfers between devices with their start and end apart: 20, of which 7 were waited for; matrix products, arithmetic and copies ran while one was open for 0% of the time, Pallas kernels for 3%

commit v1 on v0

--- a/solution.py
+++ b/solution.py
@@ -161,14 +161,15 @@
     steps = groups * per
     low = lax.broadcasted_iota(jnp.int32, (depth, 128), 1) < 64
     x, y, core, z = seat()
+    rows = pl.ds(pl.multiple_of(pl.program_id(0) * depth, depth), depth)
     for n, (r, d) in enumerate(ROUNDS):
         for h in range(2):
             came = lax.rem(core + h, 2)
             time = lax.rem(z - x + r + 2 * came + SIDE, SIDE)
             if h == 0:
-                held_ref[came, time, d] = stay_refs[n][0]
+                held_ref[came, time, d] = stay_refs[n][0, :, rows]
             else:
-                held_ref[came, time, d] = swap_refs[0][n] if n < SOON else swap_refs[1][n - SOON]
+                held_ref[came, time, d] = swap_refs[0][n, :, rows] if n < SOON else swap_refs[1][n - SOON, :, rows]
 
     def band(d, _):
         lanes = pl.ds(pl.multiple_of(lax.bitwise_xor(y, d) * 128, 128), 128)
@@ -242,8 +243,7 @@
     return pl.pallas_call(
         chain_kernel,
         grid=(depth // rows,),
-        in_specs=[pl.BlockSpec((1, 6, rows, 128), lambda s: (0, 0, s, 0))] * len(stay)
-        + [pl.BlockSpec((part.shape[0], 6, rows, 128), lambda s: (0, 0, s, 0)) for part in swap]
+        in_specs=[VMEM] * (len(stay) + len(swap))
         + [spec(6), spec(), spec(), spec(), spec(3), spec(3, CX)],
         out_specs=[spec(steps, 3), spec(3, CX)],
         out_shape=[

time: 101 us -> 100 us (0.990)
  no operation moved by 1% of the time
where the time goes in v1:
time: 100 us; the launch traced here: 99.9 us
  starting transfers between devices  59.3 us (59%)
  waiting for transfers between devices  22 us (22%)
  Pallas kernels  13 us (13%)
  local copies, waits for them, and re-layouts  4.29 us (4%)
  between operations  1.01 us (1%)
    ppermute x16, starting transfers between devices, exchange(): got.append(lax.ppermute(block, AXES, pairs))  41.3 us
    ppermute x16, waiting for transfers between devices, exchange(): got.append(lax.ppermute(block, AXES, pairs))  20.7 us
    ppermute x2, starting transfers between devices, body(): swap.append(lax.ppermute(jnp.stack([a[1] for a in part]), AXES, other))  11.5 us
    pallas_call x1, Pallas kernels, march_cells(): pl.pallas_call(chain_kernel, grid=(depth // rows,), in_specs=[VMEM] * (le...  7.14 us
    ppermute x1, starting transfers between devices, body(): before = lax.ppermute(flat[:, rows - FW:], 'tile', up)  4.58 us
    pallas_call x1, Pallas kernels, filter_rows(): pl.pallas_call(rows_kernel, in_specs=[VMEM] * 5, out_specs=[VMEM] * len(s...  3.1 us
    unnamed x33, local copies, waits for them, and re-layouts  2.92 us
    pallas_call x1, Pallas kernels, span_planes(): pl.pallas_call(span_kernel, grid=(per,), in_specs=[pl.BlockSpec((1, rows,...  2.76 us
  transfers between devices with their start and end apart: 20, of which 7 were waited for; matrix products, arithmetic and copies ran while one was open for 0% of the time, Pallas kernels for 3%

profile of v1, /device:TPU:1, one launch (start us, length us, event | category | flops | bytes accessed | tf_op | source)
XLA Modules:
  0.0 99.9 jit_solution(9490129507256716291)
XLA Ops:
  0.6 1.3 %fusion = (bf16[12,4,2048]{2,1,0:T(4,128)(2,1)S(1)}, bf16[12,4,2048]{2,1,0:T(4,128)(2,1)S(1)}) fusion(bf16[12,64,2048]{2,1,0:T(8,128)(2,1)} %bitcast.4), kind=kLoop, calls=%fused_computation.14 | loop fusion | bytes 786432 | tf_op jit(solution)/shard_map/slice | solution.py:286
  2.0 4.6 %collective-permute-start = (bf16[12,4,2048]{2,1,0:T(4,128)(2,1)S(1)}, bf16[12,4,2048]{2,1,0:T(4,128)(2,1)S(1)}, u32[]{:S(2)}, u32[]{:S(2)}) collective-permute-start(bf16[12,4,2048]{2,1,0:T(4,128)(2,1)S(1)} %get-tuple-element.34), channel_id=1, source_target_pairs={{0,1},{1,2},{2,3},{3,4},{4,5},{5,6},{6,7},{7,8},{8,9},{9,10},{10,1... | collective-permute-start | bytes 589832 | tf_op jit(solution)/shard_map/ppermute | solution.py:286
  6.6 1.9 %collective-permute-start.1 = (bf16[12,4,2048]{2,1,0:T(4,128)(2,1)S(1)}, bf16[12,4,2048]{2,1,0:T(4,128)(2,1)S(1)}, u32[]{:S(2)}, u32[]{:S(2)}) collective-permute-start(bf16[12,4,2048]{2,1,0:T(4,128)(2,1)S(1)} %get-tuple-element.35), channel_id=1, source_target_pairs={{1,0},{2,1},{3,2},{4,3},{5,4},{6,5},{7,6},{8,7},{9,8},{10,9},{11,1... | collective-permute-start | bytes 589832 | tf_op jit(solution)/shard_map/ppermute | solution.py:287
  8.5 0.0 copy-start
  8.5 1.9 %copy-done = bf16[4,3,64,2048]{3,2,1,0:T(8,128)(2,1)S(1)} copy-done((bf16[4,3,64,2048]{3,2,1,0:T(8,128)(2,1)S(1)}, bf16[4,3,64,2048]{3,2,1,0:T(8,128)(2,1)}, u32[]{:S(2)}) %copy-start) | copy-done | bytes 3145752
  10.4 0.8 copy-done.4
  11.2 2.8 %span.1.spans_ref = bf16[4,2048,192]{2,1,0:T(8,128)(2,1)S(1)} custom-call(bf16[4,192,2048]{2,1,0:T(8,128)(2,1)S(1)} %bitcast.5, bf16[128,256]{1,0:T(8,128)(2,1)S(1)} %copy-done.4), custom_call_target="tpu_custom_call" | custom-call | flops 2000000000 | bytes 4000000 | tf_op jit(solution)/shard_map/span/pallas_call | solution.py:79
  14.0 0.2 maximum_bitcast_fusion.edges_ref
  14.3 3.1 %rows.1 = (bf16[2,6,64,128]{3,2,1,0:T(8,128)(2,1)S(1)}, bf16[2,6,64,128]{3,2,1,0:T(8,128)(2,1)S(1)}, bf16[2,6,64,128]{3,2,1,0:T(8,128)(2,1)S(1)}, bf16[2,6,64,12...) custom-call(bf16[4,2048,192]{2,1,0:T(8,128)(2,1)S(1)} %span.1.spans_, ...), custom_call_target="tpu_custom_call" | custom-call | flops 1000000000 | bytes 4000000 | tf_op jit(solution)/shard_map/rows/pallas_call | solution.py:142
  17.4 4.7 %collective-permute-start.2 = (bf16[2,6,64,128]{3,2,1,0:T(8,128)(2,1)S(1)}, bf16[2,6,64,128]{3,2,1,0:T(8,128)(2,1)S(1)}, u32[]{:S(2)}, u32[]{:S(2)}) collective-permute-start(bf16[2,6,64,128]{3,2,1,0:T(8,128)(2,1)S(1)} %get-tuple-element.18), channel_id=1, source_target_pairs={{0,0},{32,24},{64,16},{96,8},{1,17},{33,9},{65,1},{97,25},{2,2},{3... | collective-permute-start | bytes 589832 | tf_op jit(solution)/shard_map/ppermute | solution.py:276
  22.1 8.1 %collective-permute-start.3 = (bf16[2,6,64,128]{3,2,1,0:T(8,128)(2,1)S(1)}, bf16[2,6,64,128]{3,2,1,0:T(8,128)(2,1)S(1)}, u32[]{:S(2)}, u32[]{:S(2)}) collective-permute-start(bf16[2,6,64,128]{3,2,1,0:T(8,128)(2,1)S(1)} %get-tuple-element.19), channel_id=1, source_target_pairs={{0,14},{32,6},{64,30},{96,22},{1,31},{33,23},{65,15},{97,7},{2,12}... | collective-permute-start | bytes 589832 | tf_op jit(solution)/shard_map/ppermute | solution.py:276
  30.1 3.3 %collective-permute-start.6 = (bf16[2,6,64,128]{3,2,1,0:T(8,128)(2,1)S(1)}, bf16[2,6,64,128]{3,2,1,0:T(8,128)(2,1)S(1)}, u32[]{:S(2)}, u32[]{:S(2)}) collective-permute-start(bf16[2,6,64,128]{3,2,1,0:T(8,128)(2,1)S(1)} %get-tuple-element.22), channel_id=1, source_target_pairs={{0,2},{32,26},{64,18},{96,10},{1,19},{33,11},{65,3},{97,27},{2,0},... | collective-permute-start | bytes 589832 | tf_op jit(solution)/shard_map/ppermute | solution.py:276
  33.5 5.1 %collective-permute-start.7 = (bf16[2,6,64,128]{3,2,1,0:T(8,128)(2,1)S(1)}, bf16[2,6,64,128]{3,2,1,0:T(8,128)(2,1)S(1)}, u32[]{:S(2)}, u32[]{:S(2)}) collective-permute-start(bf16[2,6,64,128]{3,2,1,0:T(8,128)(2,1)S(1)} %get-tuple-element.23), channel_id=1, source_target_pairs={{0,8},{32,0},{64,24},{96,16},{1,25},{33,17},{65,9},{97,1},{2,10},{... | collective-permute-start | bytes 589832 | tf_op jit(solution)/shard_map/ppermute | solution.py:276
  38.6 0.1 collective-permute-start.8
  38.7 5.5 %collective-permute-done.4.refs_2_ = bf16[2,6,64,128]{3,2,1,0:T(8,128)(2,1)S(1)} collective-permute-done((bf16[2,6,64,128]{3,2,1,0:T(8,128)(2,1)S(1)}, bf16[2,6,64,128]{3,2,1,0:T(8,128)(2,1)S(1)}, u32[]{:S(2)}, u32[]{:S(2)}) %collective-permute-start.4) | collective-permute-done | bytes 196640 | tf_op jit(solution)/shard_map/ppermute | solution.py:276
  44.2 3.3 %collective-permute-start.10 = (bf16[2,6,64,128]{3,2,1,0:T(8,128)(2,1)S(1)}, bf16[2,6,64,128]{3,2,1,0:T(8,128)(2,1)S(1)}, u32[]{:S(2)}, u32[]{:S(2)}) collective-permute-start(bf16[2,6,64,128]{3,2,1,0:T(8,128)(2,1)S(1)} %get-tuple-element.26), channel_id=1, source_target_pairs={{0,4},{32,28},{64,20},{96,12},{1,21},{33,13},{65,5},{97,29},{2,6},... | collective-permute-start | bytes 589832 | tf_op jit(solution)/shard_map/ppermute | solution.py:276
  47.6 1.3 %collective-permute-start.11 = (bf16[2,6,64,128]{3,2,1,0:T(8,128)(2,1)S(1)}, bf16[2,6,64,128]{3,2,1,0:T(8,128)(2,1)S(1)}, u32[]{:S(2)}, u32[]{:S(2)}) collective-permute-start(bf16[2,6,64,128]{3,2,1,0:T(8,128)(2,1)S(1)} %get-tuple-element.27), channel_id=1, source_target_pairs={{0,10},{32,2},{64,26},{96,18},{1,27},{33,19},{65,11},{97,3},{2,8},... | collective-permute-start | bytes 589832 | tf_op jit(solution)/shard_map/ppermute | solution.py:276
  48.9 0.8 collective-permute-start.12
  49.8 4.3 %collective-permute-start.13 = (bf16[2,6,64,128]{3,2,1,0:T(8,128)(2,1)S(1)}, bf16[2,6,64,128]{3,2,1,0:T(8,128)(2,1)S(1)}, u32[]{:S(2)}, u32[]{:S(2)}) collective-permute-start(bf16[2,6,64,128]{3,2,1,0:T(8,128)(2,1)S(1)} %get-tuple-element.29), channel_id=1, source_target_pairs={{0,30},{32,22},{64,14},{96,6},{1,15},{33,7},{65,31},{97,23},{2,28}... | collective-permute-start | bytes 589832 | tf_op jit(solution)/shard_map/ppermute | solution.py:276
  54.1 7.0 %collective-permute-done.9.refs_7_ = bf16[2,6,64,128]{3,2,1,0:T(8,128)(2,1)S(1)} collective-permute-done((bf16[2,6,64,128]{3,2,1,0:T(8,128)(2,1)S(1)}, bf16[2,6,64,128]{3,2,1,0:T(8,128)(2,1)S(1)}, u32[]{:S(2)}, u32[]{:S(2)}) %collective-permute-start.9) | collective-permute-done | bytes 196640 | tf_op jit(solution)/shard_map/ppermute | solution.py:276
  61.2 1.6 %collective-permute-done.13.refs_11_ = bf16[2,6,64,128]{3,2,1,0:T(8,128)(2,1)S(1)} collective-permute-done((bf16[2,6,64,128]{3,2,1,0:T(8,128)(2,1)S(1)}, bf16[2,6,64,128]{3,2,1,0:T(8,128)(2,1)S(1)}, u32[]{:S(2)}, u32[]{:S(2)}) %collective-permute-start.13) | collective-permute-done | bytes 196640 | tf_op jit(solution)/shard_map/ppermute | solution.py:276
  62.7 7.9 %collective-permute-start.18 = (bf16[12,6,64,128]{3,2,1,0:T(8,128)(2,1)S(1)}, bf16[12,6,64,128]{3,2,1,0:T(8,128)(2,1)S(1)}, u32[]{:S(2)}, u32[]{:S(2)}) collective-permute-start(bf16[12,6,64,128]{3,2,1,0:T(8,128)(2,1)S(1)} %slice_dynamic-update-slice_fusion), channel_id=1, source_target_pairs={{0,1},{32,33},{64,65},{96,97},{1,0},{33,32},{65,64},{97,96},{2,3},... | collective-permute-start | bytes 3538952 | tf_op jit(solution)/shard_map/ppermute | solution.py:295
  70.6 1.7 %collective-permute-start.14 = (bf16[2,6,64,128]{3,2,1,0:T(8,128)(2,1)S(1)}, bf16[2,6,64,128]{3,2,1,0:T(8,128)(2,1)S(1)}, u32[]{:S(2)}, u32[]{:S(2)}) collective-permute-start(bf16[2,6,64,128]{3,2,1,0:T(8,128)(2,1)S(1)} %get-tuple-element.30), channel_id=1, source_target_pairs={{0,6},{32,30},{64,22},{96,14},{1,23},{33,15},{65,7},{97,31},{2,4},... | collective-permute-start | bytes 589832 | tf_op jit(solution)/shard_map/ppermute | solution.py:276
  72.4 5.3 %collective-permute-start.15 = (bf16[2,6,64,128]{3,2,1,0:T(8,128)(2,1)S(1)}, bf16[2,6,64,128]{3,2,1,0:T(8,128)(2,1)S(1)}, u32[]{:S(2)}, u32[]{:S(2)}) collective-permute-start(bf16[2,6,64,128]{3,2,1,0:T(8,128)(2,1)S(1)} %get-tuple-element.31), channel_id=1, source_target_pairs={{0,12},{32,4},{64,28},{96,20},{1,29},{33,21},{65,13},{97,5},{2,14}... | collective-permute-start | bytes 589832 | tf_op jit(solution)/shard_map/ppermute | solution.py:276
  77.7 3.3 %collective-permute-start.17 = (bf16[2,6,64,128]{3,2,1,0:T(8,128)(2,1)S(1)}, bf16[2,6,64,128]{3,2,1,0:T(8,128)(2,1)S(1)}, u32[]{:S(2)}, u32[]{:S(2)}) collective-permute-start(bf16[2,6,64,128]{3,2,1,0:T(8,128)(2,1)S(1)} %get-tuple-element.33), channel_id=1, source_target_pairs={{0,24},{32,16},{64,8},{96,0},{1,9},{33,1},{65,25},{97,17},{2,26},{... | collective-permute-start | bytes 589832 | tf_op jit(solution)/shard_map/ppermute | solution.py:276
  81.0 2.2 %collective-permute-done.15.refs_13_ = bf16[2,6,64,128]{3,2,1,0:T(8,128)(2,1)S(1)} collective-permute-done((bf16[2,6,64,128]{3,2,1,0:T(8,128)(2,1)S(1)}, bf16[2,6,64,128]{3,2,1,0:T(8,128)(2,1)S(1)}, u32[]{:S(2)}, u32[]{:S(2)}) %collective-permute-start.15) | collective-permute-done | bytes 196640 | tf_op jit(solution)/shard_map/ppermute | solution.py:276
  83.2 3.9 %collective-permute-done.16.refs_14_ = bf16[2,6,64,128]{3,2,1,0:T(8,128)(2,1)S(1)} collective-permute-done((bf16[2,6,64,128]{3,2,1,0:T(8,128)(2,1)S(1)}, bf16[2,6,64,128]{3,2,1,0:T(8,128)(2,1)S(1)}, u32[]{:S(2)}, u32[]{:S(2)}) %collective-permute-start.16) | collective-permute-done | bytes 196640 | tf_op jit(solution)/shard_map/ppermute | solution.py:276
  87.2 0.5 collective-permute-done.17.refs_15_
  87.6 0.1 pad_maximum_fusion
  87.7 3.6 %collective-permute-start.19 = (bf16[4,6,64,128]{3,2,1,0:T(8,128)(2,1)S(1)}, bf16[4,6,64,128]{3,2,1,0:T(8,128)(2,1)S(1)}, u32[]{:S(2)}, u32[]{:S(2)}) collective-permute-start(bf16[4,6,64,128]{3,2,1,0:T(8,128)(2,1)S(1)} %pad_maximum_fusion), channel_id=1, source_target_pairs={{0,1},{32,33},{64,65},{96,97},{1,0},{33,32},{65,64},{97,96},{2,3},... | collective-permute-start | bytes 1179656 | tf_op jit(solution)/shard_map/ppermute | solution.py:295
  91.3 1.3 %collective-permute-done.19.refs_17_ = bf16[4,6,64,128]{3,2,1,0:T(8,128)(2,1)S(1)} collective-permute-done((bf16[4,6,64,128]{3,2,1,0:T(8,128)(2,1)S(1)}, bf16[4,6,64,128]{3,2,1,0:T(8,128)(2,1)S(1)}, u32[]{:S(2)}, u32[]{:S(2)}) %collective-permute-start.19) | collective-permute-done | bytes 393248 | tf_op jit(solution)/shard_map/ppermute | solution.py:295
  92.7 7.1 %march.1 = (bf16[16,3,64,512]{3,2,1,0:T(8,128)(2,1)}, f32[3,8,64,512]{3,2,1,0:T(8,128)}) custom-call(bf16[2,6,64,128]{3,2,1,0:T(8,128)(2,1)S(1)} %collective-permute-done.2.refs_0_, bf16[2,6,64,128]{3,2,1,0:T(8,128)(2,1)S(1)} %collective-permute-done.3.refs_1_, bf16[2,6,64,128]{3,2,1,0:T(8,128)(2,1)S(1)} %collective-permute-done.4.refs_2_, ...), custom_call_target="tpu_custom_call" | custom-call | flops 1000000000 | bytes 14000000 | tf_op jit(solution)/shard_map/march/pallas_call | solution.py:243
  (52 shorter events, 0.3 us)
Async XLA Ops:
  2.0 12.0 %collective-permute-start = (bf16[12,4,2048]{2,1,0:T(4,128)(2,1)S(1)}, bf16[12,4,2048]{2,1,0:T(4,128)(2,1)S(1)}, u32[]{:S(2)}, u32[]{:S(2)}) collective-permute-start(bf16[12,4,2048]{2,1,0:T(4,128)(2,1)S(1)} %get-tuple-element.34), channel_id=1, source_target_pairs={{0,1},{1,2},{2,3},{3,4},{4,5},{5,6},{6,7},{7,8},{8,9},{9,10},{10,1... | collective-permute-start | bytes 589832 | tf_op jit(solution)/shard_map/ppermute | solution.py:286
  6.6 7.5 %collective-permute-start.1 = (bf16[12,4,2048]{2,1,0:T(4,128)(2,1)S(1)}, bf16[12,4,2048]{2,1,0:T(4,128)(2,1)S(1)}, u32[]{:S(2)}, u32[]{:S(2)}) collective-permute-start(bf16[12,4,2048]{2,1,0:T(4,128)(2,1)S(1)} %get-tuple-element.35), channel_id=1, source_target_pairs={{1,0},{2,1},{3,2},{4,3},{5,4},{6,5},{7,6},{8,7},{9,8},{10,9},{11,1... | collective-permute-start | bytes 589832 | tf_op jit(solution)/shard_map/ppermute | solution.py:287
  8.5 1.9 %copy-start = (bf16[4,3,64,2048]{3,2,1,0:T(8,128)(2,1)S(1)}, bf16[4,3,64,2048]{3,2,1,0:T(8,128)(2,1)}, u32[]{:S(2)}) copy-start(bf16[4,3,64,2048]{3,2,1,0:T(8,128)(2,1)} %param.10) | copy-start | bytes 9437188
  10.4 0.8 copy-start.4
  11.2 3.0 %copy-start.5 = (bf16[128,256]{1,0:T(8,128)(2,1)S(1)}, bf16[128,256]{1,0:T(8,128)(2,1)}, u32[]{:S(2)}) copy-start(bf16[128,256]{1,0:T(8,128)(2,1)} %constant.6.clone.band_ref) | copy-start | bytes 196612
  11.2 3.0 %copy-start.6 = (bf16[4,96,256]{2,1,0:T(8,128)(2,1)S(1)}, bf16[4,96,256]{2,1,0:T(8,128)(2,1)}, u32[]{:S(2)}) copy-start(bf16[4,96,256]{2,1,0:T(8,128)(2,1)} %constant.8.clone.halo_ref) | copy-start | bytes 589828
  11.2 3.0 %copy-start.7 = (bf16[2,192,256]{2,1,0:T(8,128)(2,1)S(1)}, bf16[2,192,256]{2,1,0:T(8,128)(2,1)}, u32[]{:S(2)}) copy-start(bf16[2,192,256]{2,1,0:T(8,128)(2,1)} %constant.7.clone.own_ref) | copy-start | bytes 589828
  14.2 78.4 %copy-start.3 = (f32[3,64,512]{2,1,0:T(8,128)S(1)}, f32[3,64,512]{2,1,0:T(8,128)}, u32[]{:S(2)}) copy-start(f32[3,64,512]{2,1,0:T(8,128)} %refs_22_.1) | copy-start | bytes 1179652
  14.3 78.4 %copy-start.8 = (f32[64,512]{1,0:T(8,128)S(1)}, f32[64,512]{1,0:T(8,128)}, u32[]{:S(2)}) copy-start(f32[64,512]{1,0:T(8,128)} %refs_19_.1) | copy-start | bytes 393220
  14.3 78.4 %copy-start.9 = (f32[64,512]{1,0:T(8,128)S(1)}, f32[64,512]{1,0:T(8,128)}, u32[]{:S(2)}) copy-start(f32[64,512]{1,0:T(8,128)} %refs_20_.1) | copy-start | bytes 393220
  14.3 78.4 %copy-start.10 = (f32[64,512]{1,0:T(8,128)S(1)}, f32[64,512]{1,0:T(8,128)}, u32[]{:S(2)}) copy-start(f32[64,512]{1,0:T(8,128)} %refs_21_.1) | copy-start | bytes 393220
  17.4 16.1 %collective-permute-start.2 = (bf16[2,6,64,128]{3,2,1,0:T(8,128)(2,1)S(1)}, bf16[2,6,64,128]{3,2,1,0:T(8,128)(2,1)S(1)}, u32[]{:S(2)}, u32[]{:S(2)}) collective-permute-start(bf16[2,6,64,128]{3,2,1,0:T(8,128)(2,1)S(1)} %get-tuple-element.18), channel_id=1, source_target_pairs={{0,0},{32,24},{64,16},{96,8},{1,17},{33,9},{65,1},{97,25},{2,2},{3... | collective-permute-start | bytes 589832 | tf_op jit(solution)/shard_map/ppermute | solution.py:276
  22.1 16.5 %collective-permute-start.3 = (bf16[2,6,64,128]{3,2,1,0:T(8,128)(2,1)S(1)}, bf16[2,6,64,128]{3,2,1,0:T(8,128)(2,1)S(1)}, u32[]{:S(2)}, u32[]{:S(2)}) collective-permute-start(bf16[2,6,64,128]{3,2,1,0:T(8,128)(2,1)S(1)} %get-tuple-element.19), channel_id=1, source_target_pairs={{0,14},{32,6},{64,30},{96,22},{1,31},{33,23},{65,15},{97,7},{2,12}... | collective-permute-start | bytes 589832 | tf_op jit(solution)/shard_map/ppermute | solution.py:276
  30.1 14.1 %collective-permute-start.4 = (bf16[2,6,64,128]{3,2,1,0:T(8,128)(2,1)S(1)}, bf16[2,6,64,128]{3,2,1,0:T(8,128)(2,1)S(1)}, u32[]{:S(2)}, u32[]{:S(2)}) collective-permute-start(bf16[2,6,64,128]{3,2,1,0:T(8,128)(2,1)S(1)} %get-tuple-element.20), channel_id=1, source_target_pairs={{0,20},{32,12},{64,4},{96,28},{1,5},{33,29},{65,21},{97,13},{2,22}... | collective-permute-start | bytes 589832 | tf_op jit(solution)/shard_map/ppermute | solution.py:276
  30.1 14.1 %collective-permute-start.5 = (bf16[2,6,64,128]{3,2,1,0:T(8,128)(2,1)S(1)}, bf16[2,6,64,128]{3,2,1,0:T(8,128)(2,1)S(1)}, u32[]{:S(2)}, u32[]{:S(2)}) collective-permute-start(bf16[2,6,64,128]{3,2,1,0:T(8,128)(2,1)S(1)} %get-tuple-element.21), channel_id=1, source_target_pairs={{0,26},{32,18},{64,10},{96,2},{1,11},{33,3},{65,27},{97,19},{2,24}... | collective-permute-start | bytes 589832 | tf_op jit(solution)/shard_map/ppermute | solution.py:276
  30.1 17.5 %collective-permute-start.6 = (bf16[2,6,64,128]{3,2,1,0:T(8,128)(2,1)S(1)}, bf16[2,6,64,128]{3,2,1,0:T(8,128)(2,1)S(1)}, u32[]{:S(2)}, u32[]{:S(2)}) collective-permute-start(bf16[2,6,64,128]{3,2,1,0:T(8,128)(2,1)S(1)} %get-tuple-element.22), channel_id=1, source_target_pairs={{0,2},{32,26},{64,18},{96,10},{1,19},{33,11},{65,3},{97,27},{2,0},... | collective-permute-start | bytes 589832 | tf_op jit(solution)/shard_map/ppermute | solution.py:276
  33.5 15.5 %collective-permute-start.7 = (bf16[2,6,64,128]{3,2,1,0:T(8,128)(2,1)S(1)}, bf16[2,6,64,128]{3,2,1,0:T(8,128)(2,1)S(1)}, u32[]{:S(2)}, u32[]{:S(2)}) collective-permute-start(bf16[2,6,64,128]{3,2,1,0:T(8,128)(2,1)S(1)} %get-tuple-element.23), channel_id=1, source_target_pairs={{0,8},{32,0},{64,24},{96,16},{1,25},{33,17},{65,9},{97,1},{2,10},{... | collective-permute-start | bytes 589832 | tf_op jit(solution)/shard_map/ppermute | solution.py:276
  38.5 54.2 %copy-start.2 = (f32[6,64,512]{2,1,0:T(8,128)S(1)}, f32[6,64,512]{2,1,0:T(8,128)}, u32[]{:S(2)}) copy-start(f32[6,64,512]{2,1,0:T(8,128)} %refs_18_.1) | copy-start | bytes 2359300
  38.6 11.2 %collective-permute-start.8 = (bf16[2,6,64,128]{3,2,1,0:T(8,128)(2,1)S(1)}, bf16[2,6,64,128]{3,2,1,0:T(8,128)(2,1)S(1)}, u32[]{:S(2)}, u32[]{:S(2)}) collective-permute-start(bf16[2,6,64,128]{3,2,1,0:T(8,128)(2,1)S(1)} %get-tuple-element.24), channel_id=1, source_target_pairs={{0,22},{32,14},{64,6},{96,30},{1,7},{33,31},{65,23},{97,15},{2,20}... | collective-permute-start | bytes 589832 | tf_op jit(solution)/shard_map/ppermute | solution.py:276
  44.2 16.8 %collective-permute-start.9 = (bf16[2,6,64,128]{3,2,1,0:T(8,128)(2,1)S(1)}, bf16[2,6,64,128]{3,2,1,0:T(8,128)(2,1)S(1)}, u32[]{:S(2)}, u32[]{:S(2)}) collective-permute-start(bf16[2,6,64,128]{3,2,1,0:T(8,128)(2,1)S(1)} %get-tuple-element.25), channel_id=1, source_target_pairs={{0,28},{32,20},{64,12},{96,4},{1,13},{33,5},{65,29},{97,21},{2,30}... | collective-permute-start | bytes 589832 | tf_op jit(solution)/shard_map/ppermute | solution.py:276
  44.2 16.8 %collective-permute-start.10 = (bf16[2,6,64,128]{3,2,1,0:T(8,128)(2,1)S(1)}, bf16[2,6,64,128]{3,2,1,0:T(8,128)(2,1)S(1)}, u32[]{:S(2)}, u32[]{:S(2)}) collective-permute-start(bf16[2,6,64,128]{3,2,1,0:T(8,128)(2,1)S(1)} %get-tuple-element.26), channel_id=1, source_target_pairs={{0,4},{32,28},{64,20},{96,12},{1,21},{33,13},{65,5},{97,29},{2,6},... | collective-permute-start | bytes 589832 | tf_op jit(solution)/shard_map/ppermute | solution.py:276
  47.6 13.5 %collective-permute-start.11 = (bf16[2,6,64,128]{3,2,1,0:T(8,128)(2,1)S(1)}, bf16[2,6,64,128]{3,2,1,0:T(8,128)(2,1)S(1)}, u32[]{:S(2)}, u32[]{:S(2)}) collective-permute-start(bf16[2,6,64,128]{3,2,1,0:T(8,128)(2,1)S(1)} %get-tuple-element.27), channel_id=1, source_target_pairs={{0,10},{32,2},{64,26},{96,18},{1,27},{33,19},{65,11},{97,3},{2,8},... | collective-permute-start | bytes 589832 | tf_op jit(solution)/shard_map/ppermute | solution.py:276
  48.9 43.8 %copy-start.1 = (f32[3,8,64,512]{3,2,1,0:T(8,128)S(1)}, f32[3,8,64,512]{3,2,1,0:T(8,128)}, u32[]{:S(2)}) copy-start(f32[3,8,64,512]{3,2,1,0:T(8,128)} %refs_23_.1) | copy-start | bytes 9437188
  48.9 12.2 %collective-permute-start.12 = (bf16[2,6,64,128]{3,2,1,0:T(8,128)(2,1)S(1)}, bf16[2,6,64,128]{3,2,1,0:T(8,128)(2,1)S(1)}, u32[]{:S(2)}, u32[]{:S(2)}) collective-permute-start(bf16[2,6,64,128]{3,2,1,0:T(8,128)(2,1)S(1)} %get-tuple-element.28), channel_id=1, source_target_pairs={{0,16},{32,8},{64,0},{96,24},{1,1},{33,25},{65,17},{97,9},{2,18},{... | collective-permute-start | bytes 589832 | tf_op jit(solution)/shard_map/ppermute | solution.py:276
  49.8 12.9 %collective-permute-start.13 = (bf16[2,6,64,128]{3,2,1,0:T(8,128)(2,1)S(1)}, bf16[2,6,64,128]{3,2,1,0:T(8,128)(2,1)S(1)}, u32[]{:S(2)}, u32[]{:S(2)}) collective-permute-start(bf16[2,6,64,128]{3,2,1,0:T(8,128)(2,1)S(1)} %get-tuple-element.29), channel_id=1, source_target_pairs={{0,30},{32,22},{64,14},{96,6},{1,15},{33,7},{65,31},{97,23},{2,28}... | collective-permute-start | bytes 589832 | tf_op jit(solution)/shard_map/ppermute | solution.py:276
  62.7 29.9 %collective-permute-start.18 = (bf16[12,6,64,128]{3,2,1,0:T(8,128)(2,1)S(1)}, bf16[12,6,64,128]{3,2,1,0:T(8,128)(2,1)S(1)}, u32[]{:S(2)}, u32[]{:S(2)}) collective-permute-start(bf16[12,6,64,128]{3,2,1,0:T(8,128)(2,1)S(1)} %slice_dynamic-update-slice_fusion), channel_id=1, source_target_pairs={{0,1},{32,33},{64,65},{96,97},{1,0},{33,32},{65,64},{97,96},{2,3},... | collective-permute-start | bytes 3538952 | tf_op jit(solution)/shard_map/ppermute | solution.py:295
  70.6 10.4 %collective-permute-start.14 = (bf16[2,6,64,128]{3,2,1,0:T(8,128)(2,1)S(1)}, bf16[2,6,64,128]{3,2,1,0:T(8,128)(2,1)S(1)}, u32[]{:S(2)}, u32[]{:S(2)}) collective-permute-start(bf16[2,6,64,128]{3,2,1,0:T(8,128)(2,1)S(1)} %get-tuple-element.30), channel_id=1, source_target_pairs={{0,6},{32,30},{64,22},{96,14},{1,23},{33,15},{65,7},{97,31},{2,4},... | collective-permute-start | bytes 589832 | tf_op jit(solution)/shard_map/ppermute | solution.py:276
  72.4 10.9 %collective-permute-start.15 = (bf16[2,6,64,128]{3,2,1,0:T(8,128)(2,1)S(1)}, bf16[2,6,64,128]{3,2,1,0:T(8,128)(2,1)S(1)}, u32[]{:S(2)}, u32[]{:S(2)}) collective-permute-start(bf16[2,6,64,128]{3,2,1,0:T(8,128)(2,1)S(1)} %get-tuple-element.31), channel_id=1, source_target_pairs={{0,12},{32,4},{64,28},{96,20},{1,29},{33,21},{65,13},{97,5},{2,14}... | collective-permute-start | bytes 589832 | tf_op jit(solution)/shard_map/ppermute | solution.py:276
  77.7 9.4 %collective-permute-start.16 = (bf16[2,6,64,128]{3,2,1,0:T(8,128)(2,1)S(1)}, bf16[2,6,64,128]{3,2,1,0:T(8,128)(2,1)S(1)}, u32[]{:S(2)}, u32[]{:S(2)}) collective-permute-start(bf16[2,6,64,128]{3,2,1,0:T(8,128)(2,1)S(1)} %get-tuple-element.32), channel_id=1, source_target_pairs={{0,18},{32,10},{64,2},{96,26},{1,3},{33,27},{65,19},{97,11},{2,16}... | collective-permute-start | bytes 589832 | tf_op jit(solution)/shard_map/ppermute | solution.py:276
  77.7 9.9 %collective-permute-start.17 = (bf16[2,6,64,128]{3,2,1,0:T(8,128)(2,1)S(1)}, bf16[2,6,64,128]{3,2,1,0:T(8,128)(2,1)S(1)}, u32[]{:S(2)}, u32[]{:S(2)}) collective-permute-start(bf16[2,6,64,128]{3,2,1,0:T(8,128)(2,1)S(1)} %get-tuple-element.33), channel_id=1, source_target_pairs={{0,24},{32,16},{64,8},{96,0},{1,9},{33,1},{65,25},{97,17},{2,26},{... | collective-permute-start | bytes 589832 | tf_op jit(solution)/shard_map/ppermute | solution.py:276
  87.7 5.0 %collective-permute-start.19 = (bf16[4,6,64,128]{3,2,1,0:T(8,128)(2,1)S(1)}, bf16[4,6,64,128]{3,2,1,0:T(8,128)(2,1)S(1)}, u32[]{:S(2)}, u32[]{:S(2)}) collective-permute-start(bf16[4,6,64,128]{3,2,1,0:T(8,128)(2,1)S(1)} %pad_maximum_fusion), channel_id=1, source_target_pairs={{0,1},{32,33},{64,65},{96,97},{1,0},{33,32},{65,64},{97,96},{2,3},... | collective-permute-start | bytes 1179656 | tf_op jit(solution)/shard_map/ppermute | solution.py:295

commit v2 on v1

--- a/solution.py
+++ b/solution.py
@@ -61,8 +61,18 @@
 VMEM = pl.BlockSpec(memory_space=pltpu.VMEM)
 
 
-def span_kernel(noise_ref, band_ref, out_ref):
+def span_kernel(noise_ref, out_ref, band_ref):
     i = pl.program_id(0)
+
+    @pl.when(i == 0)
+    def _():
+        shape = band_ref.shape
+        index = lax.broadcasted_iota(jnp.int32, shape, 1) - lax.broadcasted_iota(jnp.int32, shape, 0) - 64 + FW
+        band = jnp.zeros(shape, F32)
+        for tap, value in enumerate(filter_taps().astype(np.float32)):
+            band = jnp.where(index == tap, float(value), band)
+        band_ref[...] = band.astype(BF16)
+
     windows = noise_ref.shape[2] // 128
     for w in range(windows):
         if w < windows - 1:
@@ -74,22 +84,23 @@
         ).astype(BF16)
 
 
-def span_planes(noise, band):
+def span_planes(noise):
     per, rows, length = noise.shape
     return pl.pallas_call(
         span_kernel,
         grid=(per,),
-        in_specs=[pl.BlockSpec((1, rows, length), lambda i: (i, 0, 0)), VMEM],
+        in_specs=[pl.BlockSpec((1, rows, length), lambda i: (i, 0, 0))],
         out_specs=VMEM,
         out_shape=jax.ShapeDtypeStruct((per, length, rows), BF16),
+        scratch_shapes=[pltpu.VMEM((128, 256), BF16)],
         compiler_params=pltpu.CompilerParams(vmem_limit_bytes=12 * 2**20),
         cost_estimate=cost(2 * 10**9, 4 * 10**6),
         name="span",
-    )(noise, band)
+    )(noise)
 
 
 ROUNDS = [(r, (d - r) % SIDE) for d in range(SIDE) for r in range(SIDE)]
-SOON = 12
+SOON = 13
 
 
 def seat():
@@ -287,7 +298,7 @@
     after = lax.ppermute(flat[:, :FW], "tile", down)
     halo = jnp.concatenate([before, after], axis=1).reshape(per * comps * 2 * FW, length)
     weights = filter_weights(per, comps, rows)
-    spans = span_planes(noise.reshape(per, comps * rows, length), weights[0])
+    spans = span_planes(noise.reshape(per, comps * rows, length))
     other = moves(lambda x, y, core, z: (x, y, 1 - core, z))
     swap = []
     got = exchange(filter_rows(spans, halo, weights))

time: 100 us -> 99.2 us (level)
  starting transfers between devices: 59.3 us -> 46 us
  waiting for transfers between devices: 22 us -> 35.1 us
    ppermute x16, waiting for transfers between devices: 20.7 us -> 33.6 us  [exchange(): got.append(lax.ppermute(block, AXES, pairs))]
    ppermute x2, starting transfers between devices: 11.5 us -> 3.97 us  [body(): swap.append(lax.ppermute(jnp.stack([a[1] for a in part]), AXES, other))]
    ppermute x16, starting transfers between devices: 41.3 us -> 35.6 us  [exchange(): got.append(lax.ppermute(block, AXES, pairs))]
    unnamed x33 -> x32, local copies, waits for them, and re-layouts: 2.92 us -> 2.1 us
  transfers between devices with their start and end apart: 20 -> 20, of which waited for: 7 -> 6; matrix products, arithmetic and copies ran while one was open for 0% -> 0% of each run, Pallas kernels for 3% -> 3%
where the time goes in v2:
time: 99.2 us; the launch traced here: 98.9 us
  starting transfers between devices  46 us (46%)
  waiting for transfers between devices  35.1 us (35%)
  Pallas kernels  13.1 us (13%)
  local copies, waits for them, and re-layouts  3.46 us (3%)
  between operations  1 us (1%)
    ppermute x16, starting transfers between devices, exchange(): got.append(lax.ppermute(block, AXES, pairs))  35.6 us
    ppermute x16, waiting for transfers between devices, exchange(): got.append(lax.ppermute(block, AXES, pairs))  33.6 us
    pallas_call x1, Pallas kernels, march_cells(): pl.pallas_call(chain_kernel, grid=(depth // rows,), in_specs=[VMEM] * (le...  7.14 us
    ppermute x1, starting transfers between devices, body(): before = lax.ppermute(flat[:, rows - FW:], 'tile', up)  4.58 us
    ppermute x2, starting transfers between devices, body(): swap.append(lax.ppermute(jnp.stack([a[1] for a in part]), AXES, other))  3.97 us
    pallas_call x1, Pallas kernels, filter_rows(): pl.pallas_call(rows_kernel, in_specs=[VMEM] * 5, out_specs=[VMEM] * len(s...  3.09 us
    pallas_call x1, Pallas kernels, span_planes(): pl.pallas_call(span_kernel, grid=(per,), in_specs=[pl.BlockSpec((1, rows,...  2.88 us
    unnamed x32, local copies, waits for them, and re-layouts  2.1 us
  transfers between devices with their start and end apart: 20, of which 6 were waited for; matrix products, arithmetic and copies ran while one was open for 0% of the time, Pallas kernels for 3%

profile of v2, /device:TPU:1, one launch (start us, length us, event | category | flops | bytes accessed | tf_op | source)
XLA Modules:
  0.0 98.9 jit_solution(3712961635917563113)
XLA Ops:
  0.6 1.3 %fusion = (bf16[12,4,2048]{2,1,0:T(4,128)(2,1)S(1)}, bf16[12,4,2048]{2,1,0:T(4,128)(2,1)S(1)}) fusion(bf16[12,64,2048]{2,1,0:T(8,128)(2,1)} %bitcast.4), kind=kLoop, calls=%fused_computation.15 | loop fusion | bytes 786432 | tf_op jit(solution)/shard_map/slice | solution.py:297
  2.0 4.6 %collective-permute-start = (bf16[12,4,2048]{2,1,0:T(4,128)(2,1)S(1)}, bf16[12,4,2048]{2,1,0:T(4,128)(2,1)S(1)}, u32[]{:S(2)}, u32[]{:S(2)}) collective-permute-start(bf16[12,4,2048]{2,1,0:T(4,128)(2,1)S(1)} %get-tuple-element.34), channel_id=1, source_target_pairs={{0,1},{1,2},{2,3},{3,4},{4,5},{5,6},{6,7},{7,8},{8,9},{9,10},{10,1... | collective-permute-start | bytes 589832 | tf_op jit(solution)/shard_map/ppermute | solution.py:297
  6.6 1.9 %collective-permute-start.1 = (bf16[12,4,2048]{2,1,0:T(4,128)(2,1)S(1)}, bf16[12,4,2048]{2,1,0:T(4,128)(2,1)S(1)}, u32[]{:S(2)}, u32[]{:S(2)}) collective-permute-start(bf16[12,4,2048]{2,1,0:T(4,128)(2,1)S(1)} %get-tuple-element.35), channel_id=1, source_target_pairs={{1,0},{2,1},{3,2},{4,3},{5,4},{6,5},{7,6},{8,7},{9,8},{10,9},{11,1... | collective-permute-start | bytes 589832 | tf_op jit(solution)/shard_map/ppermute | solution.py:298
  8.5 0.0 copy-start.9
  8.5 1.9 %copy-done.9 = bf16[4,3,64,2048]{3,2,1,0:T(8,128)(2,1)S(1)} copy-done((bf16[4,3,64,2048]{3,2,1,0:T(8,128)(2,1)S(1)}, bf16[4,3,64,2048]{3,2,1,0:T(8,128)(2,1)}, u32[]{:S(2)}) %copy-start.9) | copy-done | bytes 3145752
  10.4 2.9 %span.1.spans_ref = bf16[4,2048,192]{2,1,0:T(8,128)(2,1)S(1)} custom-call(bf16[4,192,2048]{2,1,0:T(8,128)(2,1)S(1)} %bitcast.5), custom_call_target="tpu_custom_call" | custom-call | flops 2000000000 | bytes 4000000 | tf_op jit(solution)/shard_map/span/pallas_call | solution.py:89
  13.3 0.3 collective-permute-done.1
  13.5 0.2 maximum_bitcast_fusion.edges_ref
  13.8 0.0 copy-start.1
  13.8 0.0 copy-start.6
  13.8 0.0 copy-start.7
  13.8 3.1 %rows.1 = (bf16[2,6,64,128]{3,2,1,0:T(8,128)(2,1)S(1)}, bf16[2,6,64,128]{3,2,1,0:T(8,128)(2,1)S(1)}, bf16[2,6,64,128]{3,2,1,0:T(8,128)(2,1)S(1)}, bf16[2,6,64,12...) custom-call(bf16[4,2048,192]{2,1,0:T(8,128)(2,1)S(1)} %span.1.spans_, ...), custom_call_target="tpu_custom_call" | custom-call | flops 1000000000 | bytes 4000000 | tf_op jit(solution)/shard_map/rows/pallas_call | solution.py:153
  16.9 4.7 %collective-permute-start.2 = (bf16[2,6,64,128]{3,2,1,0:T(8,128)(2,1)S(1)}, bf16[2,6,64,128]{3,2,1,0:T(8,128)(2,1)S(1)}, u32[]{:S(2)}, u32[]{:S(2)}) collective-permute-start(bf16[2,6,64,128]{3,2,1,0:T(8,128)(2,1)S(1)} %get-tuple-element.18), channel_id=1, source_target_pairs={{0,0},{32,24},{64,16},{96,8},{1,17},{33,9},{65,1},{97,25},{2,2},{3... | collective-permute-start | bytes 589832 | tf_op jit(solution)/shard_map/ppermute | solution.py:287
  21.6 8.5 %collective-permute-start.3 = (bf16[2,6,64,128]{3,2,1,0:T(8,128)(2,1)S(1)}, bf16[2,6,64,128]{3,2,1,0:T(8,128)(2,1)S(1)}, u32[]{:S(2)}, u32[]{:S(2)}) collective-permute-start(bf16[2,6,64,128]{3,2,1,0:T(8,128)(2,1)S(1)} %get-tuple-element.19), channel_id=1, source_target_pairs={{0,14},{32,6},{64,30},{96,22},{1,31},{33,23},{65,15},{97,7},{2,12}... | collective-permute-start | bytes 589832 | tf_op jit(solution)/shard_map/ppermute | solution.py:287
  30.1 2.8 %collective-permute-start.6 = (bf16[2,6,64,128]{3,2,1,0:T(8,128)(2,1)S(1)}, bf16[2,6,64,128]{3,2,1,0:T(8,128)(2,1)S(1)}, u32[]{:S(2)}, u32[]{:S(2)}) collective-permute-start(bf16[2,6,64,128]{3,2,1,0:T(8,128)(2,1)S(1)} %get-tuple-element.22), channel_id=1, source_target_pairs={{0,2},{32,26},{64,18},{96,10},{1,19},{33,11},{65,3},{97,27},{2,0},... | collective-permute-start | bytes 589832 | tf_op jit(solution)/shard_map/ppermute | solution.py:287
  33.0 5.6 %collective-permute-start.7 = (bf16[2,6,64,128]{3,2,1,0:T(8,128)(2,1)S(1)}, bf16[2,6,64,128]{3,2,1,0:T(8,128)(2,1)S(1)}, u32[]{:S(2)}, u32[]{:S(2)}) collective-permute-start(bf16[2,6,64,128]{3,2,1,0:T(8,128)(2,1)S(1)} %get-tuple-element.23), channel_id=1, source_target_pairs={{0,8},{32,0},{64,24},{96,16},{1,25},{33,17},{65,9},{97,1},{2,10},{... | collective-permute-start | bytes 589832 | tf_op jit(solution)/shard_map/ppermute | solution.py:287
  38.5 0.0 copy-start.5
  38.6 0.6 collective-permute-start.8
  39.2 5.4 %collective-permute-done.4.refs_2_ = bf16[2,6,64,128]{3,2,1,0:T(8,128)(2,1)S(1)} collective-permute-done((bf16[2,6,64,128]{3,2,1,0:T(8,128)(2,1)S(1)}, bf16[2,6,64,128]{3,2,1,0:T(8,128)(2,1)S(1)}, u32[]{:S(2)}, u32[]{:S(2)}) %collective-permute-start.4) | collective-permute-done | bytes 196640 | tf_op jit(solution)/shard_map/ppermute | solution.py:287
  44.6 2.5 %collective-permute-start.10 = (bf16[2,6,64,128]{3,2,1,0:T(8,128)(2,1)S(1)}, bf16[2,6,64,128]{3,2,1,0:T(8,128)(2,1)S(1)}, u32[]{:S(2)}, u32[]{:S(2)}) collective-permute-start(bf16[2,6,64,128]{3,2,1,0:T(8,128)(2,1)S(1)} %get-tuple-element.26), channel_id=1, source_target_pairs={{0,4},{32,28},{64,20},{96,12},{1,21},{33,13},{65,5},{97,29},{2,6},... | collective-permute-start | bytes 589832 | tf_op jit(solution)/shard_map/ppermute | solution.py:287
  47.1 1.2 %collective-permute-start.11 = (bf16[2,6,64,128]{3,2,1,0:T(8,128)(2,1)S(1)}, bf16[2,6,64,128]{3,2,1,0:T(8,128)(2,1)S(1)}, u32[]{:S(2)}, u32[]{:S(2)}) collective-permute-start(bf16[2,6,64,128]{3,2,1,0:T(8,128)(2,1)S(1)} %get-tuple-element.27), channel_id=1, source_target_pairs={{0,10},{32,2},{64,26},{96,18},{1,27},{33,19},{65,11},{97,3},{2,8},... | collective-permute-start | bytes 589832 | tf_op jit(solution)/shard_map/ppermute | solution.py:287
  48.4 0.7 collective-permute-start.12
  49.1 4.1 %collective-permute-start.13 = (bf16[2,6,64,128]{3,2,1,0:T(8,128)(2,1)S(1)}, bf16[2,6,64,128]{3,2,1,0:T(8,128)(2,1)S(1)}, u32[]{:S(2)}, u32[]{:S(2)}) collective-permute-start(bf16[2,6,64,128]{3,2,1,0:T(8,128)(2,1)S(1)} %get-tuple-element.29), channel_id=1, source_target_pairs={{0,30},{32,22},{64,14},{96,6},{1,15},{33,7},{65,31},{97,23},{2,28}... | collective-permute-start | bytes 589832 | tf_op jit(solution)/shard_map/ppermute | solution.py:287
  53.2 8.4 %collective-permute-done.9.refs_7_ = bf16[2,6,64,128]{3,2,1,0:T(8,128)(2,1)S(1)} collective-permute-done((bf16[2,6,64,128]{3,2,1,0:T(8,128)(2,1)S(1)}, bf16[2,6,64,128]{3,2,1,0:T(8,128)(2,1)S(1)}, u32[]{:S(2)}, u32[]{:S(2)}) %collective-permute-start.9) | collective-permute-done | bytes 196640 | tf_op jit(solution)/shard_map/ppermute | solution.py:287
  61.7 9.7 %collective-permute-done.14.refs_12_ = bf16[2,6,64,128]{3,2,1,0:T(8,128)(2,1)S(1)} collective-permute-done((bf16[2,6,64,128]{3,2,1,0:T(8,128)(2,1)S(1)}, bf16[2,6,64,128]{3,2,1,0:T(8,128)(2,1)S(1)}, u32[]{:S(2)}, u32[]{:S(2)}) %collective-permute-start.14) | collective-permute-done | bytes 196640 | tf_op jit(solution)/shard_map/ppermute | solution.py:287
  71.4 1.8 %collective-permute-start.18 = (bf16[13,6,64,128]{3,2,1,0:T(8,128)(2,1)S(1)}, bf16[13,6,64,128]{3,2,1,0:T(8,128)(2,1)S(1)}, u32[]{:S(2)}, u32[]{:S(2)}) collective-permute-start(bf16[13,6,64,128]{3,2,1,0:T(8,128)(2,1)S(1)} %slice_dynamic-update-slice_fusion), channel_id=1, source_target_pairs={{0,1},{32,33},{64,65},{96,97},{1,0},{33,32},{65,64},{97,96},{2,3},... | collective-permute-start | bytes 3833864 | tf_op jit(solution)/shard_map/ppermute | solution.py:306
  73.2 1.8 %collective-permute-start.15 = (bf16[2,6,64,128]{3,2,1,0:T(8,128)(2,1)S(1)}, bf16[2,6,64,128]{3,2,1,0:T(8,128)(2,1)S(1)}, u32[]{:S(2)}, u32[]{:S(2)}) collective-permute-start(bf16[2,6,64,128]{3,2,1,0:T(8,128)(2,1)S(1)} %get-tuple-element.31), channel_id=1, source_target_pairs={{0,12},{32,4},{64,28},{96,20},{1,29},{33,21},{65,13},{97,5},{2,14}... | collective-permute-start | bytes 589832 | tf_op jit(solution)/shard_map/ppermute | solution.py:287
  75.0 3.1 %collective-permute-start.17 = (bf16[2,6,64,128]{3,2,1,0:T(8,128)(2,1)S(1)}, bf16[2,6,64,128]{3,2,1,0:T(8,128)(2,1)S(1)}, u32[]{:S(2)}, u32[]{:S(2)}) collective-permute-start(bf16[2,6,64,128]{3,2,1,0:T(8,128)(2,1)S(1)} %get-tuple-element.33), channel_id=1, source_target_pairs={{0,24},{32,16},{64,8},{96,0},{1,9},{33,1},{65,25},{97,17},{2,26},{... | collective-permute-start | bytes 589832 | tf_op jit(solution)/shard_map/ppermute | solution.py:287
  78.0 10.2 %collective-permute-done.15.refs_13_ = bf16[2,6,64,128]{3,2,1,0:T(8,128)(2,1)S(1)} collective-permute-done((bf16[2,6,64,128]{3,2,1,0:T(8,128)(2,1)S(1)}, bf16[2,6,64,128]{3,2,1,0:T(8,128)(2,1)S(1)}, u32[]{:S(2)}, u32[]{:S(2)}) %collective-permute-start.15) | collective-permute-done | bytes 196640 | tf_op jit(solution)/shard_map/ppermute | solution.py:287
  88.3 2.2 %collective-permute-start.19 = (bf16[3,6,64,128]{3,2,1,0:T(8,128)(2,1)S(1)}, bf16[3,6,64,128]{3,2,1,0:T(8,128)(2,1)S(1)}, u32[]{:S(2)}, u32[]{:S(2)}) collective-permute-start(bf16[3,6,64,128]{3,2,1,0:T(8,128)(2,1)S(1)} %pad_maximum_fusion), channel_id=1, source_target_pairs={{0,1},{32,33},{64,65},{96,97},{1,0},{33,32},{65,64},{97,96},{2,3},... | collective-permute-start | bytes 884744 | tf_op jit(solution)/shard_map/ppermute | solution.py:306
  90.6 1.2 %collective-permute-done.19.refs_17_ = bf16[3,6,64,128]{3,2,1,0:T(8,128)(2,1)S(1)} collective-permute-done((bf16[3,6,64,128]{3,2,1,0:T(8,128)(2,1)S(1)}, bf16[3,6,64,128]{3,2,1,0:T(8,128)(2,1)S(1)}, u32[]{:S(2)}, u32[]{:S(2)}) %collective-permute-start.19) | collective-permute-done | bytes 294944 | tf_op jit(solution)/shard_map/ppermute | solution.py:306
  91.8 7.1 %march.1 = (bf16[16,3,64,512]{3,2,1,0:T(8,128)(2,1)}, f32[3,8,64,512]{3,2,1,0:T(8,128)}) custom-call(bf16[2,6,64,128]{3,2,1,0:T(8,128)(2,1)S(1)} %collective-permute-done.2.refs_0_, bf16[2,6,64,128]{3,2,1,0:T(8,128)(2,1)S(1)} %collective-permute-done.3.refs_1_, bf16[2,6,64,128]{3,2,1,0:T(8,128)(2,1)S(1)} %collective-permute-done.4.refs_2_, ...), custom_call_target="tpu_custom_call" | custom-call | flops 1000000000 | bytes 14000000 | tf_op jit(solution)/shard_map/march/pallas_call | solution.py:254
  (50 shorter events, 0.3 us)
Async XLA Ops:
  2.0 11.3 %collective-permute-start = (bf16[12,4,2048]{2,1,0:T(4,128)(2,1)S(1)}, bf16[12,4,2048]{2,1,0:T(4,128)(2,1)S(1)}, u32[]{:S(2)}, u32[]{:S(2)}) collective-permute-start(bf16[12,4,2048]{2,1,0:T(4,128)(2,1)S(1)} %get-tuple-element.34), channel_id=1, source_target_pairs={{0,1},{1,2},{2,3},{3,4},{4,5},{5,6},{6,7},{7,8},{8,9},{9,10},{10,1... | collective-permute-start | bytes 589832 | tf_op jit(solution)/shard_map/ppermute | solution.py:297
  6.6 7.0 %collective-permute-start.1 = (bf16[12,4,2048]{2,1,0:T(4,128)(2,1)S(1)}, bf16[12,4,2048]{2,1,0:T(4,128)(2,1)S(1)}, u32[]{:S(2)}, u32[]{:S(2)}) collective-permute-start(bf16[12,4,2048]{2,1,0:T(4,128)(2,1)S(1)} %get-tuple-element.35), channel_id=1, source_target_pairs={{1,0},{2,1},{3,2},{4,3},{5,4},{6,5},{7,6},{8,7},{9,8},{10,9},{11,1... | collective-permute-start | bytes 589832 | tf_op jit(solution)/shard_map/ppermute | solution.py:298
  8.5 1.9 %copy-start.9 = (bf16[4,3,64,2048]{3,2,1,0:T(8,128)(2,1)S(1)}, bf16[4,3,64,2048]{3,2,1,0:T(8,128)(2,1)}, u32[]{:S(2)}) copy-start(bf16[4,3,64,2048]{3,2,1,0:T(8,128)(2,1)} %param.10) | copy-start | bytes 9437188
  10.4 3.4 %copy-start.3 = (bf16[4,96,256]{2,1,0:T(8,128)(2,1)S(1)}, bf16[4,96,256]{2,1,0:T(8,128)(2,1)}, u32[]{:S(2)}) copy-start(bf16[4,96,256]{2,1,0:T(8,128)(2,1)} %constant.8.clone.halo_ref) | copy-start | bytes 589828
  10.4 3.4 %copy-start.4 = (bf16[2,192,256]{2,1,0:T(8,128)(2,1)S(1)}, bf16[2,192,256]{2,1,0:T(8,128)(2,1)}, u32[]{:S(2)}) copy-start(bf16[2,192,256]{2,1,0:T(8,128)(2,1)} %constant.7.clone.own_ref) | copy-start | bytes 589828
  10.4 3.4 %copy-start.8 = (bf16[128,256]{1,0:T(8,128)(2,1)S(1)}, bf16[128,256]{1,0:T(8,128)(2,1)}, u32[]{:S(2)}) copy-start(bf16[128,256]{1,0:T(8,128)(2,1)} %constant.6.clone.band_ref) | copy-start | bytes 196612
  13.8 78.0 %copy-start.1 = (f32[6,64,512]{2,1,0:T(8,128)S(1)}, f32[6,64,512]{2,1,0:T(8,128)}, u32[]{:S(2)}) copy-start(f32[6,64,512]{2,1,0:T(8,128)} %refs_18_.1) | copy-start | bytes 2359300
  13.8 78.0 %copy-start.6 = (f32[64,512]{1,0:T(8,128)S(1)}, f32[64,512]{1,0:T(8,128)}, u32[]{:S(2)}) copy-start(f32[64,512]{1,0:T(8,128)} %refs_20_.1) | copy-start | bytes 393220
  13.8 78.0 %copy-start.7 = (f32[64,512]{1,0:T(8,128)S(1)}, f32[64,512]{1,0:T(8,128)}, u32[]{:S(2)}) copy-start(f32[64,512]{1,0:T(8,128)} %refs_21_.1) | copy-start | bytes 393220
  16.9 16.1 %collective-permute-start.2 = (bf16[2,6,64,128]{3,2,1,0:T(8,128)(2,1)S(1)}, bf16[2,6,64,128]{3,2,1,0:T(8,128)(2,1)S(1)}, u32[]{:S(2)}, u32[]{:S(2)}) collective-permute-start(bf16[2,6,64,128]{3,2,1,0:T(8,128)(2,1)S(1)} %get-tuple-element.18), channel_id=1, source_target_pairs={{0,0},{32,24},{64,16},{96,8},{1,17},{33,9},{65,1},{97,25},{2,2},{3... | collective-permute-start | bytes 589832 | tf_op jit(solution)/shard_map/ppermute | solution.py:287
  21.6 17.0 %collective-permute-start.3 = (bf16[2,6,64,128]{3,2,1,0:T(8,128)(2,1)S(1)}, bf16[2,6,64,128]{3,2,1,0:T(8,128)(2,1)S(1)}, u32[]{:S(2)}, u32[]{:S(2)}) collective-permute-start(bf16[2,6,64,128]{3,2,1,0:T(8,128)(2,1)S(1)} %get-tuple-element.19), channel_id=1, source_target_pairs={{0,14},{32,6},{64,30},{96,22},{1,31},{33,23},{65,15},{97,7},{2,12}... | collective-permute-start | bytes 589832 | tf_op jit(solution)/shard_map/ppermute | solution.py:287
  30.1 14.5 %collective-permute-start.4 = (bf16[2,6,64,128]{3,2,1,0:T(8,128)(2,1)S(1)}, bf16[2,6,64,128]{3,2,1,0:T(8,128)(2,1)S(1)}, u32[]{:S(2)}, u32[]{:S(2)}) collective-permute-start(bf16[2,6,64,128]{3,2,1,0:T(8,128)(2,1)S(1)} %get-tuple-element.20), channel_id=1, source_target_pairs={{0,20},{32,12},{64,4},{96,28},{1,5},{33,29},{65,21},{97,13},{2,22}... | collective-permute-start | bytes 589832 | tf_op jit(solution)/shard_map/ppermute | solution.py:287
  30.1 14.5 %collective-permute-start.5 = (bf16[2,6,64,128]{3,2,1,0:T(8,128)(2,1)S(1)}, bf16[2,6,64,128]{3,2,1,0:T(8,128)(2,1)S(1)}, u32[]{:S(2)}, u32[]{:S(2)}) collective-permute-start(bf16[2,6,64,128]{3,2,1,0:T(8,128)(2,1)S(1)} %get-tuple-element.21), channel_id=1, source_target_pairs={{0,26},{32,18},{64,10},{96,2},{1,11},{33,3},{65,27},{97,19},{2,24}... | collective-permute-start | bytes 589832 | tf_op jit(solution)/shard_map/ppermute | solution.py:287
  30.1 17.0 %collective-permute-start.6 = (bf16[2,6,64,128]{3,2,1,0:T(8,128)(2,1)S(1)}, bf16[2,6,64,128]{3,2,1,0:T(8,128)(2,1)S(1)}, u32[]{:S(2)}, u32[]{:S(2)}) collective-permute-start(bf16[2,6,64,128]{3,2,1,0:T(8,128)(2,1)S(1)} %get-tuple-element.22), channel_id=1, source_target_pairs={{0,2},{32,26},{64,18},{96,10},{1,19},{33,11},{65,3},{97,27},{2,0},... | collective-permute-start | bytes 589832 | tf_op jit(solution)/shard_map/ppermute | solution.py:287
  33.0 15.4 %collective-permute-start.7 = (bf16[2,6,64,128]{3,2,1,0:T(8,128)(2,1)S(1)}, bf16[2,6,64,128]{3,2,1,0:T(8,128)(2,1)S(1)}, u32[]{:S(2)}, u32[]{:S(2)}) collective-permute-start(bf16[2,6,64,128]{3,2,1,0:T(8,128)(2,1)S(1)} %get-tuple-element.23), channel_id=1, source_target_pairs={{0,8},{32,0},{64,24},{96,16},{1,25},{33,17},{65,9},{97,1},{2,10},{... | collective-permute-start | bytes 589832 | tf_op jit(solution)/shard_map/ppermute | solution.py:287
  38.5 53.2 %copy-start.5 = (f32[64,512]{1,0:T(8,128)S(1)}, f32[64,512]{1,0:T(8,128)}, u32[]{:S(2)}) copy-start(f32[64,512]{1,0:T(8,128)} %refs_19_.1) | copy-start | bytes 393220
  38.6 10.5 %collective-permute-start.8 = (bf16[2,6,64,128]{3,2,1,0:T(8,128)(2,1)S(1)}, bf16[2,6,64,128]{3,2,1,0:T(8,128)(2,1)S(1)}, u32[]{:S(2)}, u32[]{:S(2)}) collective-permute-start(bf16[2,6,64,128]{3,2,1,0:T(8,128)(2,1)S(1)} %get-tuple-element.24), channel_id=1, source_target_pairs={{0,22},{32,14},{64,6},{96,30},{1,7},{33,31},{65,23},{97,15},{2,20}... | collective-permute-start | bytes 589832 | tf_op jit(solution)/shard_map/ppermute | solution.py:287
  39.2 52.6 %copy-start.2 = (f32[3,64,512]{2,1,0:T(8,128)S(1)}, f32[3,64,512]{2,1,0:T(8,128)}, u32[]{:S(2)}) copy-start(f32[3,64,512]{2,1,0:T(8,128)} %refs_22_.1) | copy-start | bytes 1179652
  44.6 17.0 %collective-permute-start.9 = (bf16[2,6,64,128]{3,2,1,0:T(8,128)(2,1)S(1)}, bf16[2,6,64,128]{3,2,1,0:T(8,128)(2,1)S(1)}, u32[]{:S(2)}, u32[]{:S(2)}) collective-permute-start(bf16[2,6,64,128]{3,2,1,0:T(8,128)(2,1)S(1)} %get-tuple-element.25), channel_id=1, source_target_pairs={{0,28},{32,20},{64,12},{96,4},{1,13},{33,5},{65,29},{97,21},{2,30}... | collective-permute-start | bytes 589832 | tf_op jit(solution)/shard_map/ppermute | solution.py:287
  44.6 17.0 %collective-permute-start.10 = (bf16[2,6,64,128]{3,2,1,0:T(8,128)(2,1)S(1)}, bf16[2,6,64,128]{3,2,1,0:T(8,128)(2,1)S(1)}, u32[]{:S(2)}, u32[]{:S(2)}) collective-permute-start(bf16[2,6,64,128]{3,2,1,0:T(8,128)(2,1)S(1)} %get-tuple-element.26), channel_id=1, source_target_pairs={{0,4},{32,28},{64,20},{96,12},{1,21},{33,13},{65,5},{97,29},{2,6},... | collective-permute-start | bytes 589832 | tf_op jit(solution)/shard_map/ppermute | solution.py:287
  47.1 44.7 %copy-start = (f32[3,8,64,512]{3,2,1,0:T(8,128)S(1)}, f32[3,8,64,512]{3,2,1,0:T(8,128)}, u32[]{:S(2)}) copy-start(f32[3,8,64,512]{3,2,1,0:T(8,128)} %refs_23_.1) | copy-start | bytes 9437188
  47.1 14.5 %collective-permute-start.11 = (bf16[2,6,64,128]{3,2,1,0:T(8,128)(2,1)S(1)}, bf16[2,6,64,128]{3,2,1,0:T(8,128)(2,1)S(1)}, u32[]{:S(2)}, u32[]{:S(2)}) collective-permute-start(bf16[2,6,64,128]{3,2,1,0:T(8,128)(2,1)S(1)} %get-tuple-element.27), channel_id=1, source_target_pairs={{0,10},{32,2},{64,26},{96,18},{1,27},{33,19},{65,11},{97,3},{2,8},... | collective-permute-start | bytes 589832 | tf_op jit(solution)/shard_map/ppermute | solution.py:287
  48.4 13.3 %collective-permute-start.12 = (bf16[2,6,64,128]{3,2,1,0:T(8,128)(2,1)S(1)}, bf16[2,6,64,128]{3,2,1,0:T(8,128)(2,1)S(1)}, u32[]{:S(2)}, u32[]{:S(2)}) collective-permute-start(bf16[2,6,64,128]{3,2,1,0:T(8,128)(2,1)S(1)} %get-tuple-element.28), channel_id=1, source_target_pairs={{0,16},{32,8},{64,0},{96,24},{1,1},{33,25},{65,17},{97,9},{2,18},{... | collective-permute-start | bytes 589832 | tf_op jit(solution)/shard_map/ppermute | solution.py:287
  49.1 12.6 %collective-permute-start.13 = (bf16[2,6,64,128]{3,2,1,0:T(8,128)(2,1)S(1)}, bf16[2,6,64,128]{3,2,1,0:T(8,128)(2,1)S(1)}, u32[]{:S(2)}, u32[]{:S(2)}) collective-permute-start(bf16[2,6,64,128]{3,2,1,0:T(8,128)(2,1)S(1)} %get-tuple-element.29), channel_id=1, source_target_pairs={{0,30},{32,22},{64,14},{96,6},{1,15},{33,7},{65,31},{97,23},{2,28}... | collective-permute-start | bytes 589832 | tf_op jit(solution)/shard_map/ppermute | solution.py:287
  61.6 9.8 %collective-permute-start.14 = (bf16[2,6,64,128]{3,2,1,0:T(8,128)(2,1)S(1)}, bf16[2,6,64,128]{3,2,1,0:T(8,128)(2,1)S(1)}, u32[]{:S(2)}, u32[]{:S(2)}) collective-permute-start(bf16[2,6,64,128]{3,2,1,0:T(8,128)(2,1)S(1)} %get-tuple-element.30), channel_id=1, source_target_pairs={{0,6},{32,30},{64,22},{96,14},{1,23},{33,15},{65,7},{97,31},{2,4},... | collective-permute-start | bytes 589832 | tf_op jit(solution)/shard_map/ppermute | solution.py:287
  71.4 20.3 %collective-permute-start.18 = (bf16[13,6,64,128]{3,2,1,0:T(8,128)(2,1)S(1)}, bf16[13,6,64,128]{3,2,1,0:T(8,128)(2,1)S(1)}, u32[]{:S(2)}, u32[]{:S(2)}) collective-permute-start(bf16[13,6,64,128]{3,2,1,0:T(8,128)(2,1)S(1)} %slice_dynamic-update-slice_fusion), channel_id=1, source_target_pairs={{0,1},{32,33},{64,65},{96,97},{1,0},{33,32},{65,64},{97,96},{2,3},... | collective-permute-start | bytes 3833864 | tf_op jit(solution)/shard_map/ppermute | solution.py:306
  73.2 15.0 %collective-permute-start.15 = (bf16[2,6,64,128]{3,2,1,0:T(8,128)(2,1)S(1)}, bf16[2,6,64,128]{3,2,1,0:T(8,128)(2,1)S(1)}, u32[]{:S(2)}, u32[]{:S(2)}) collective-permute-start(bf16[2,6,64,128]{3,2,1,0:T(8,128)(2,1)S(1)} %get-tuple-element.31), channel_id=1, source_target_pairs={{0,12},{32,4},{64,28},{96,20},{1,29},{33,21},{65,13},{97,5},{2,14}... | collective-permute-start | bytes 589832 | tf_op jit(solution)/shard_map/ppermute | solution.py:287
  75.0 13.3 %collective-permute-start.16 = (bf16[2,6,64,128]{3,2,1,0:T(8,128)(2,1)S(1)}, bf16[2,6,64,128]{3,2,1,0:T(8,128)(2,1)S(1)}, u32[]{:S(2)}, u32[]{:S(2)}) collective-permute-start(bf16[2,6,64,128]{3,2,1,0:T(8,128)(2,1)S(1)} %get-tuple-element.32), channel_id=1, source_target_pairs={{0,18},{32,10},{64,2},{96,26},{1,3},{33,27},{65,19},{97,11},{2,16}... | collective-permute-start | bytes 589832 | tf_op jit(solution)/shard_map/ppermute | solution.py:287
  75.0 13.3 %collective-permute-start.17 = (bf16[2,6,64,128]{3,2,1,0:T(8,128)(2,1)S(1)}, bf16[2,6,64,128]{3,2,1,0:T(8,128)(2,1)S(1)}, u32[]{:S(2)}, u32[]{:S(2)}) collective-permute-start(bf16[2,6,64,128]{3,2,1,0:T(8,128)(2,1)S(1)} %get-tuple-element.33), channel_id=1, source_target_pairs={{0,24},{32,16},{64,8},{96,0},{1,9},{33,1},{65,25},{97,17},{2,26},{... | collective-permute-start | bytes 589832 | tf_op jit(solution)/shard_map/ppermute | solution.py:287
  88.3 3.4 %collective-permute-start.19 = (bf16[3,6,64,128]{3,2,1,0:T(8,128)(2,1)S(1)}, bf16[3,6,64,128]{3,2,1,0:T(8,128)(2,1)S(1)}, u32[]{:S(2)}, u32[]{:S(2)}) collective-permute-start(bf16[3,6,64,128]{3,2,1,0:T(8,128)(2,1)S(1)} %pad_maximum_fusion), channel_id=1, source_target_pairs={{0,1},{32,33},{64,65},{96,97},{1,0},{33,32},{65,64},{97,96},{2,3},... | collective-permute-start | bytes 884744 | tf_op jit(solution)/shard_map/ppermute | solution.py:306
